TPU v7x, 128 devices: a whole 4x4x4 slice. The times are simulated.
128 devices in a mesh: node: 16 (over y, x), harm: 8 (over z, core).
Axes of the slice: x: 4, y: 4, z: 4, core: 2. Of those that a mesh axis runs over, the one named last changes fastest.
Arguments:
- krylov_basis: float32 [8, 2, 64, 32768], P(None, None, 'harm', 'node'), may hold values from -100 to 100, as said below
- cond_time: float32 [64, 32768], P('harm', 'node'), may hold values from 2 to 6
- capacity: float32 [32768], P('node'), may hold values from 0.005 to 0.05
- diag_blocks: float32 [128, 256, 256], P('node'), may hold values from -1 to 1
- coupling: float32 [128, 2, 256, 256], P('node'), may hold values from -0.375 to 0.375
- neighbours: int32 [128, 2], P('node'), may hold values from 0 to 127, as said below
- pattern: int32 [128, 2], P('node'), may hold values from 0 to 1
Outputs:
- new_vector: float32 [2, 64, 32768], P(None, 'harm', 'node')
- projections: float32 [2, 8], replicated
- new_norm: float32 [], replicated
Inputs may be any that keep to these rules, and one draw needn't show every extreme that they name: `neighbours`: with the blocks in groups of 8 consecutive ones, each entry lies in a group 1 to 3 groups away from its row's group; the present slots of the rows of one group name at most 2 distinct blocks of any other group. `krylov_basis`: each of the 8 vectors has mean squared entry 1 over its real and imaginary parts.
All inputs are finite; a program needn't handle non-finite values.
Results may differ from a plain program's by a relative error of at most 0.0003.
Values sent between devices are 32-bit elements; how exact they have to be, the bound alone decides.
No kernel may reach another device: no remote copies, remote signals or barrier semaphores. Data moves between devices by JAX's collectives and lax.ppermute only.
A program may use at most 64 MiB of HBM per device.

v0:
```python
import math

import jax
import jax.numpy as jnp
import numpy as np
from jax import lax
from jax.experimental import pallas as pl
from jax.experimental.pallas import tpu as pltpu
from jax.sharding import Mesh
from jax.sharding import PartitionSpec as P

BS = 256
H = 64
NEIGH = 2
KRY = 8
HARM = ("harm_0", "harm_1")
NODE = ("node_0", "node_1")
NODE_HARM = ("node_0", "node_1", "harm_0", "harm_1")
F32 = jnp.float32
BF16 = jnp.bfloat16
LANES = 128
GRAM = 64
SMEM = pl.BlockSpec(memory_space=pltpu.SMEM)
VMEM = pl.BlockSpec(memory_space=pltpu.VMEM)


def spectral_tables():
    steps = np.arange(H)
    angles = (steps[:, None] * steps[None, :] % H) * (2.0 * math.pi / H)
    cosine = np.cos(angles) / math.sqrt(H)
    sine = np.sin(angles) / math.sqrt(H)
    table = np.block([[cosine, -sine], [sine, cosine]]).astype(np.float32)
    both = np.stack([table, table.T])
    high = both.astype(jnp.bfloat16)
    low = (both - high.astype(np.float32)).astype(jnp.bfloat16)
    return high, low


def split(x):
    high = x.astype(BF16)
    return high, (x - high.astype(F32)).astype(BF16)


def mm(a, b):
    return jnp.dot(a, b, preferred_element_type=F32)


def mm_t(a, b):
    return lax.dot_general(a, b, (((1,), (1,)), ((), ())), preferred_element_type=F32)


def rows_mm(x, w_high, w_low, product=mm):
    rows = x.shape[0]
    high, low = split(x)
    both = product(jnp.concatenate([high, low], axis=0), w_high)
    return both[:rows] + both[rows:] + product(high, w_low)


def sublane_sum(x):
    return jnp.sum(x, axis=0, keepdims=True)


def rows_to_lanes(rows):
    return sublane_sum(jnp.transpose(rows))


def pack_kernel(nb_ref, pat_ref, v_ref, cond_ref, out_ref, hot_ref):
    blk = out_ref.shape[0]
    sums = jnp.concatenate(
        [sublane_sum(cond_ref[:, BS * b : BS * (b + 1)]) for b in range(blk)], axis=0
    )
    for b in range(blk):
        cols = slice(BS * b, BS * (b + 1))
        out_ref[b, 0] = v_ref[0, 0, :, cols]
        out_ref[b, 1] = v_ref[0, 1, :, cols]
        out_ref[b, 2] = cond_ref[:, cols]
        out_ref[b, 3] = sums
    groups = hot_ref.shape[0]
    for q in range(groups):
        hot_ref[q, 0] = blk
        hot_ref[q, 1] = -1
    for b in range(blk):
        for j in range(NEIGH):
            block = nb_ref[b, j]
            group = block // blk
            local = block - group * blk

            @pl.when(pat_ref[b, j] > 0)
            def _():
                hot_ref[group, 0] = jnp.minimum(hot_ref[group, 0], local)
                hot_ref[group, 1] = jnp.maximum(hot_ref[group, 1], local)


def prep_kernel(diag_ref, k_ref, t_ref, gram_ref, rows):
    for b in range(diag_ref.shape[0]):
        t_ref[b] = jnp.transpose(diag_ref[b])
    rows[...] = jnp.zeros_like(rows)
    chunks = k_ref.shape[3] // LANES
    for m in range(KRY):
        real = [None] * KRY
        imag = [None] * KRY
        for c in range(chunks):
            cols = slice(LANES * c, LANES * (c + 1))
            mr, mi = k_ref[m, 0, :, cols], k_ref[m, 1, :, cols]
            for n in range(m, KRY):
                nr, ni = (mr, mi) if n == m else (k_ref[n, 0, :, cols], k_ref[n, 1, :, cols])
                r = mr * nr + mi * ni
                real[n] = r if c == 0 else real[n] + r
                if n > m:
                    i = mr * ni - mi * nr
                    imag[n] = i if c == 0 else imag[n] + i
        for n in range(m, KRY):
            at = GRAM + KRY * m + n
            rows[at : at + 1] = sublane_sum(real[n])
            if n > m:
                at = GRAM + KRY * n + m
                rows[at : at + 1] = sublane_sum(imag[n])
    gram_ref[...] = rows_to_lanes(rows[...])


def solve_kernel(place_ref, hot_ref, got_ref, t_ref, v_ref, send_ref, own_ref, means_ref, e_ref, row_ref, d_ref):
    blk = t_ref.shape[0]
    half = v_ref.shape[2]
    means = got_ref[0, 3]
    for s in range(1, got_ref.shape[0]):
        means = means + got_ref[s, 3]
    means = means * (1.0 / H)
    means_ref[...] = means
    d_ref[...] = 1.0 / means

    def one(b):
        d = d_ref[pl.ds(b, 1), :]
        cols = pl.ds(pl.multiple_of(b * BS, BS), BS)
        power = t_ref[b] * (-d)
        u = jnp.concatenate([v_ref[0, 0, :, cols], v_ref[0, 1, :, cols]], axis=0) * d
        for p in range(4):
            high, low = split(power)
            e_ref[b, p, 0] = high
            e_ref[b, p, 1] = low
            u = u + rows_mm(u, high, low)
            if p < 3:
                both = mm(jnp.concatenate([high, low], axis=0), high)
                power = both[:BS] + both[BS:] + mm(high, low)
        row_ref[b, 0] = u[:half]
        row_ref[b, 1] = u[half:]

    def pair(i, carry):
        one(2 * i)
        one(2 * i + 1)
        return carry

    lax.fori_loop(0, blk // 2, pair, 0)

    me = place_ref[0]
    own = place_ref[1]
    own_ref[...] = e_ref[own]
    groups = send_ref.shape[0]
    for q in range(groups):
        send_ref[q] = jnp.zeros(send_ref.shape[1:], F32)
    for offset in (1, 2, 3, -1, -2, -3):
        group = me + offset

        @pl.when((group >= 0) & (group < groups))
        def _():
            first = jnp.minimum(hot_ref[group, 0], blk - 1)
            second = jnp.maximum(hot_ref[group, 1], 0)
            send_ref[group, 0:2] = row_ref[first]
            send_ref[group, 2:4] = row_ref[second]


def column_kernel(place_ref, got_ref, own_ref, means_ref, cap_ref, omega_ref, high_ref, low_ref, out_ref):
    sources = got_ref.shape[0]
    own = place_ref[1]
    mean = means_ref[pl.ds(own, 1), :]
    u = jnp.concatenate([got_ref[s, p] for p in range(2) for s in range(sources)], axis=0)
    u = u * (1.0 / mean)
    for p in range(4):
        u = u + rows_mm(u, own_ref[p, 0], own_ref[p, 1])
    direct = rows_mm(u, own_ref[0, 0], own_ref[0, 1]) * (-mean)

    def transform(way, x):
        high, low = split(x)
        table = high_ref[way]
        return mm(table, high) + mm(table, low) + mm(low_ref[way], high)

    cond = jnp.concatenate([got_ref[s, 2] for s in range(sources)], axis=0)
    driven = transform(0, u) * jnp.concatenate([cond, cond], axis=0)
    image = direct + transform(1, driven)
    react = omega_ref[...] * cap_ref[pl.ds(own, 1), :]
    real = image[:H] - react * u[H:]
    imag = image[H:] + react * u[:H]
    step = H // sources
    for s in range(sources):
        out_ref[s, 0] = real[step * s : step * (s + 1)]
        out_ref[s, 1] = imag[step * s : step * (s + 1)]


def image_kernel(nb_ref, pat_ref, hot_ref, back_ref, got_ref, c_ref, k_ref, gram_ref, image_ref, send_ref, rows):
    blk = c_ref.shape[0]
    half = k_ref.shape[2]

    def one(b):
        total = jnp.concatenate([back_ref[b, 0], back_ref[b, 1]], axis=0)
        for j in range(NEIGH):
            block = nb_ref[b, j]
            group = block // blk
            second = jnp.where(block - group * blk == hot_ref[group, 0], 0, 2)
            x = jnp.concatenate([got_ref[group, second], got_ref[group, second + 1]], axis=0)
            x = x * pat_ref[b, j].astype(F32)
            total = total + rows_mm(x, *split(c_ref[b, j]), product=mm_t)
        cols = pl.ds(pl.multiple_of(b * BS, BS), BS)
        image_ref[0, :, cols] = total[:half]
        image_ref[1, :, cols] = total[half:]

    def pair(i, carry):
        one(2 * i)
        one(2 * i + 1)
        return carry

    lax.fori_loop(0, blk // 2, pair, 0)

    chunks = k_ref.shape[3] // LANES
    real = [None] * KRY
    imag = [None] * KRY
    squares = None
    for c in range(chunks):
        cols = slice(LANES * c, LANES * (c + 1))
        ir, ii = image_ref[0, :, cols], image_ref[1, :, cols]
        both = ir * ir + ii * ii
        squares = both if c == 0 else squares + both
        for m in range(KRY):
            mr, mi = k_ref[m, 0, :, cols], k_ref[m, 1, :, cols]
            r = mr * ir + mi * ii
            i = mr * ii - mi * ir
            real[m] = r if c == 0 else real[m] + r
            imag[m] = i if c == 0 else imag[m] + i
    rows[...] = jnp.zeros_like(rows)
    for m in range(KRY):
        rows[m : m + 1] = sublane_sum(real[m])
        rows[KRY + m : KRY + m + 1] = sublane_sum(imag[m])
    rows[2 * KRY : 2 * KRY + 1] = sublane_sum(squares)
    row = rows_to_lanes(rows[...]) + gram_ref[...]
    send_ref[...] = jnp.broadcast_to(row, send_ref.shape)


def rest_kernel(count, got_ref, image_ref, k_ref, vector_ref, proj_ref, norm_ref):
    totals = sublane_sum(got_ref[...]) * (1.0 / count)
    lane = lax.broadcasted_iota(jnp.int32, totals.shape, 1)

    def at(q):
        return jnp.broadcast_to(totals[:, q : q + 1], totals.shape)

    pr = [at(m) for m in range(KRY)]
    pi = [at(KRY + m) for m in range(KRY)]
    row_r = row_i = col_r = col_i = jnp.zeros_like(totals)
    row_of = (lane - GRAM) // KRY
    col_of = (lane - GRAM) - row_of * KRY
    for m in range(KRY):
        row_r = jnp.where(row_of == m, pr[m], row_r)
        row_i = jnp.where(row_of == m, pi[m], row_i)
        col_r = jnp.where(col_of == m, pr[m], col_r)
        col_i = jnp.where(col_of == m, pi[m], col_i)
    upper = row_r * col_r + row_i * col_i
    lower = col_i * row_r - col_r * row_i
    weight = jnp.where(row_of == col_of, upper, 2.0 * jnp.where(row_of < col_of, upper, lower))
    weight = jnp.where(lane >= GRAM, weight, 0.0)
    weight = jnp.where(lane < 2 * KRY, -2.0 * totals, weight)
    weight = jnp.where(lane == 2 * KRY, 1.0, weight)
    squares = jnp.sum(totals * weight, axis=1, keepdims=True)
    norm = jnp.sqrt(squares + 1e-06)
    norm_ref[...] = norm
    for m in range(KRY):
        proj_ref[0:1, m : m + 1] = pr[m][:, 0:1]
        proj_ref[1:2, m : m + 1] = pi[m][:, 0:1]
    half = k_ref.shape[2]
    scale = jnp.broadcast_to(1.0 / norm, (half, LANES))
    pr = [jnp.broadcast_to(x, (half, LANES)) for x in pr]
    pi = [jnp.broadcast_to(x, (half, LANES)) for x in pi]
    for c in range(k_ref.shape[3] // LANES):
        cols = slice(LANES * c, LANES * (c + 1))
        real, imag = image_ref[0, :, cols], image_ref[1, :, cols]
        for m in range(KRY):
            mr, mi = k_ref[m, 0, :, cols], k_ref[m, 1, :, cols]
            real = real - (pr[m] * mr - pi[m] * mi)
            imag = imag - (pr[m] * mi + pi[m] * mr)
        vector_ref[0, :, cols] = real * scale
        vector_ref[1, :, cols] = imag * scale


def struct(*dims, dtype=F32):
    return jax.ShapeDtypeStruct(dims, dtype)


def call(kernel, out_shape, in_specs, out_specs, name, flops, scratch=(), **kw):
    return pl.pallas_call(
        kernel,
        out_shape=out_shape,
        in_specs=in_specs,
        out_specs=out_specs,
        scratch_shapes=list(scratch),
        name=name,
        cost_estimate=pl.CostEstimate(flops=flops, bytes_accessed=1 << 20, transcendentals=0),
        **kw,
    )


def exchange(x, axes):
    return lax.all_to_all(x, axes, split_axis=0, concat_axis=0, tiled=True)


def per_device(krylov_basis, cond_time, capacity, diag_blocks, coupling, neighbours, pattern):
    h_dev = krylov_basis.shape[2]
    nodes_dev = krylov_basis.shape[3]
    blk = diag_blocks.shape[0]
    harm = lax.axis_size(HARM)
    groups = lax.axis_size(NODE)
    world = groups * harm
    place = jnp.stack([lax.axis_index(NODE), lax.axis_index(HARM)]).astype(jnp.int32)
    last = pl.BlockSpec((1, 2, h_dev, nodes_dev), lambda i: (KRY - 1, 0, 0, 0))

    packed, hot_own = call(
        pack_kernel,
        (struct(blk, 4, h_dev, BS), struct(groups, LANES, dtype=jnp.int32)),
        [SMEM, SMEM, last, pl.BlockSpec((h_dev, nodes_dev), lambda i: (0, 0))],
        (pl.BlockSpec((blk, 4, h_dev, BS), lambda i: (0, 0, 0, 0)), SMEM),
        "pack",
        1 << 20,
        grid=(1,),
    )(neighbours, pattern, krylov_basis, cond_time)
    got = exchange(packed, HARM)
    hot = exchange(hot_own, NODE)
    turned, gram = call(
        prep_kernel,
        (struct(blk, BS, BS), struct(1, LANES)),
        [VMEM, VMEM],
        (VMEM, VMEM),
        "prep",
        1 << 28,
        [pltpu.VMEM((LANES, LANES), F32)],
    )(diag_blocks, krylov_basis)
    whole = lambda *dims: pl.BlockSpec(dims, lambda i: (0,) * len(dims))
    send_hot, own, means = call(
        solve_kernel,
        (struct(groups, 4, h_dev, BS), struct(4, 2, BS, BS, dtype=BF16), struct(blk, BS)),
        [SMEM, SMEM, whole(harm, 4, h_dev, BS), whole(blk, BS, BS), last],
        (whole(groups, 4, h_dev, BS), whole(4, 2, BS, BS), whole(blk, BS)),
        "solve",
        1 << 31,
        [
            pltpu.VMEM((blk, 4, 2, BS, BS), BF16),
            pltpu.VMEM((blk, 2, h_dev, BS), F32),
            pltpu.VMEM((blk, BS), F32),
        ],
        grid=(1,),
    )(place, hot, got, turned, krylov_basis)
    named = exchange(send_hot, NODE)
    high, low = spectral_tables()
    omega = np.broadcast_to((((np.arange(H) + H // 2) % H) - H // 2).astype(np.float32)[:, None], (H, BS))
    send_cols = call(
        column_kernel,
        struct(harm, 2, h_dev, BS),
        [SMEM] + [VMEM] * 7,
        VMEM,
        "column",
        1 << 27,
    )(place, got, own, means, capacity.reshape(blk, BS), jnp.asarray(omega), jnp.asarray(high), jnp.asarray(low))
    back = exchange(send_cols, HARM)
    image, send_sums = call(
        image_kernel,
        (struct(2, h_dev, nodes_dev), struct(world, LANES)),
        [SMEM] * 3 + [VMEM] * 5,
        (VMEM, VMEM),
        "image",
        1 << 28,
        [pltpu.VMEM((LANES, LANES), F32)],
    )(neighbours, pattern, hot_own, back, named, coupling, krylov_basis, gram)
    sums = exchange(send_sums, NODE_HARM)
    count = world * h_dev * nodes_dev
    vector, proj, norm = call(
        lambda *refs: rest_kernel(count, *refs),
        (struct(2, h_dev, nodes_dev), struct(2, KRY), struct(1, 1)),
        [VMEM] * 3,
        (VMEM, VMEM, VMEM),
        "rest",
        1 << 24,
    )(sums, image, krylov_basis)
    return vector, proj, norm.reshape(())


def solution(mesh):
    finer = Mesh(mesh.devices.reshape(4, 4, 4, 2), ("node_0", "node_1", "harm_0", "harm_1"))
    placed = (
        P(None, None, HARM, NODE),
        P(HARM, NODE),
        P(NODE),
        P(NODE, None, None),
        P(NODE, None, None, None),
        P(NODE, None),
        P(NODE, None),
    )
    return jax.shard_map(
        per_device,
        mesh=finer,
        in_specs=placed,
        out_specs=(P(None, HARM, NODE), P(), P()),
        check_vma=False,
    )
```

profile of v0, /device:TPU:1, one launch (start us, length us, event | category | flops | bytes accessed | tf_op | source)
XLA Modules:
  0.0 98.0 jit_solution(5826320650438180164)
XLA Ops:
  0.6 1.3 %copy.20.nb_ref = s32[8,2]{1,0:T(8,128)} copy(s32[8,2]{0,1:T(2,128)} %param.15) | data formatting | bytes 128 | tf_op args[5]
  2.0 1.3 %copy.21.pat_ref = s32[8,2]{1,0:T(8,128)} copy(s32[8,2]{0,1:T(2,128)} %param.16) | data formatting | bytes 128 | tf_op args[6]
  3.3 1.8 %pack.1 = (f32[8,4,8,256]{3,2,1,0:T(8,128)}, s32[16,128]{1,0:T(8,128)}) custom-call(s32[8,2]{1,0:T(8,128)} %copy.20.nb_ref, s32[8,2]{1,0:T(8,128)} %copy.21.pat_ref, f32[8,2,8,2048]{3,2,1,0:T(8,128)} %refs_2_.1, f32[8,2048]{1,0:T(8,128)} %cond_ref.1), custom_call_target="tpu_custom_call" | custom-call | flops 1048576 | bytes 1048576 | tf_op jit(solution)/shard_map/pack/pallas_call | solution.py:321
  5.1 14.0 %all_to_all.37 = s32[16,1,128]{2,1,0:T(1,128)} all-to-all(s32[16,1,128]{2,1,0:T(1,128)} %bitcast.13), channel_id=1, replica_groups=mesh['node_0'=4,'node_1'=4,'harm_0'=4,'harm_1'=2] {'node_0','node_1'}, dimensions={0} | all-to-all | bytes 16384 | tf_op jit(solution)/shard_map/all_to_all | solution.py:308
  19.1 7.4 %all-to-all-start = ((f32[8,4,8,256]{3,2,1,0:T(8,128)}), f32[8,4,8,256]{3,2,1,0:T(8,128)S(1)}, u32[]{:S(2)}, u32[]{:S(2)}) async-start(f32[8,4,8,256]{3,2,1,0:T(8,128)} %get-tuple-element.16), calls=%async_computation | async-start | bytes 524288 | tf_op jit(solution)/shard_map/all_to_all | solution.py:308
  26.5 1.3 %reshape.16.cap_ref = f32[8,256]{1,0:T(8,128)} reshape(f32[2048]{0:T(1024)} %param.12) | data formatting | bytes 16384 | tf_op jit(solution)/shard_map/reshape | solution.py:366
  27.8 4.3 %prep.1 = (f32[8,256,256]{2,1,0:T(8,128)}, f32[1,128]{1,0:T(1,128)}) custom-call(f32[8,256,256]{2,1,0:T(8,128)} %diag_ref.1, f32[8,2,8,2048]{3,2,1,0:T(8,128)} %refs_2_.1), custom_call_target="tpu_custom_call" | custom-call | flops 268435456 | bytes 1048576 | tf_op jit(solution)/shard_map/prep/pallas_call | solution.py:332
  32.1 0.6 pad_add_fusion.place_ref
  32.7 0.2 all-to-all-done.got_ref
  32.9 0.0 copy-start
  32.9 0.7 copy-done
  33.6 0.0 copy-start.2
  33.6 12.8 %solve.1 = (f32[16,4,8,256]{3,2,1,0:T(8,128)}, bf16[4,2,256,256]{3,2,1,0:T(8,128)(2,1)}, f32[8,256]{1,0:T(8,128)}) custom-call(s32[2]{0:T(128)} %pad_add_fusion.place_ref, s32[16,128]{1,0:T(8,128)} %bitcast.14, f32[8,4,8,256]{3,2,1,0:T(8,128)} %copy-done, f32[8,256,256]{2,1,0:T(8,128)} %get-tuple-element.17.t_ref, f32[8,2,8,2048]{3,2,1,0:T(8,128)} %refs_2_.1), custom_call_target="tpu_custom_call" | custom-call | flops 2147483648 | bytes 1048576 | tf_op jit(solution)/shard_map/solve/pallas_call | solution.py:342
  46.4 0.0 copy-start.1
  46.4 0.0 copy-done.2
  46.4 0.7 jit_solution_.3.omega_ref
  47.1 3.2 %column.1 = f32[8,2,8,256]{3,2,1,0:T(8,128)} custom-call(s32[2]{0:T(128)} %pad_add_fusion.place_ref, f32[8,4,8,256]{3,2,1,0:T(8,128)} %copy-done, bf16[4,2,256,256]{3,2,1,0:T(8,128)(2,1)} %get-tuple-element.18.own_ref, f32[8,256]{1,0:T(8,128)} %get-tuple-element.19.means_ref, f32[8,256]{1,0:T(8,128)} %reshape.16.cap_ref, f32[64,256]{1,0:T(8,128)} %jit_solution_.3.omega_ref, ...), custom_call_target="tpu_custom_call" | custom-call | flops 134217728 | bytes 1048576 | tf_op jit(solution)/shard_map/column/pallas_call | solution.py:359
  50.3 10.2 %all_to_all.38.back_ref = f32[8,2,8,256]{3,2,1,0:T(8,128)} all-to-all(f32[8,2,8,256]{3,2,1,0:T(8,128)} %column.1), channel_id=1, replica_groups=mesh['node_0'=4,'node_1'=4,'harm_0'=4,'harm_1'=2] {'harm_0','harm_1'}, dimensions={0} | all-to-all | bytes 262144 | tf_op jit(solution)/shard_map/all_to_all | solution.py:308
  60.6 0.0 copy-done.1
  60.6 13.8 %all_to_all.39.got_ref = f32[16,4,8,256]{3,2,1,0:T(8,128)} all-to-all(f32[16,4,8,256]{3,2,1,0:T(8,128)S(1)} %copy-done.1), channel_id=1, replica_groups=mesh['node_0'=4,'node_1'=4,'harm_0'=4,'harm_1'=2] {'node_0','node_1'}, dimensions={0} | all-to-all | bytes 1048576 | tf_op jit(solution)/shard_map/all_to_all | solution.py:308
  74.4 5.3 %image.1 = (f32[2,8,2048]{2,1,0:T(8,128)}, f32[128,128]{1,0:T(8,128)}) custom-call(s32[8,2]{1,0:T(8,128)} %copy.20.nb_ref, s32[8,2]{1,0:T(8,128)} %copy.21.pat_ref, s32[16,128]{1,0:T(8,128)} %get-tuple-element.15.hot_ref, f32[8,2,8,256]{3,2,1,0:T(8,128)} %all_to_all.38.back_ref, f32[16,4,8,256]{3,2,1,0:T(8,128)} %all_to_all.39.got_ref, ...), custom_call_target="tpu_custom_call" | custom-call | flops 268435456 | bytes 1048576 | tf_op jit(solution)/shard_map/image/pallas_call | solution.py:368
  79.6 16.1 %all_to_all.40 = f32[128,1,128]{2,1,0:T(1,128)} all-to-all(f32[128,1,128]{2,1,0:T(1,128)} %bitcast.12), channel_id=1, replica_groups=mesh['node_0'=4,'node_1'=4,'harm_0'=4,'harm_1'=2] {'node_0','node_1','ha..., dimensions={0} | all-to-all | bytes 131072 | tf_op jit(solution)/shard_map/all_to_all | solution.py:308
  95.8 2.3 %rest.1 = (f32[2,8,2048]{2,1,0:T(8,128)}, f32[2,8]{1,0:T(2,128)}, f32[1,1]{1,0:T(1,128)}) custom-call(f32[128,128]{1,0:T(8,128)} %bitcast.11, f32[2,8,2048]{2,1,0:T(8,128)} %get-tuple-element.23.refs_1_, f32[8,2,8,2048]{3,2,1,0:T(8,128)} %refs_2_.1), custom_call_target="tpu_custom_call" | custom-call | flops 16777216 | bytes 1048576 | tf_op jit(solution)/shard_map/rest/pallas_call | solution.py:379
Async XLA Ops:
  19.1 13.9 %all-to-all-start = ((f32[8,4,8,256]{3,2,1,0:T(8,128)}), f32[8,4,8,256]{3,2,1,0:T(8,128)S(1)}, u32[]{:S(2)}, u32[]{:S(2)}) async-start(f32[8,4,8,256]{3,2,1,0:T(8,128)} %get-tuple-element.16), calls=%async_computation | async-start | bytes 524288 | tf_op jit(solution)/shard_map/all_to_all | solution.py:308
  32.9 0.7 copy-start
  33.6 12.8 %copy-start.2 = (f32[64]{0:T(128)S(1)}, f32[64]{0:T(128)}, u32[]{:S(2)}) copy-start(f32[64]{0:T(128)} %constant.25.clone) | copy-start | bytes 772
  46.4 14.2 %copy-start.1 = (f32[16,4,8,256]{3,2,1,0:T(8,128)S(1)}, f32[16,4,8,256]{3,2,1,0:T(8,128)}, u32[]{:S(2)}) copy-start(f32[16,4,8,256]{3,2,1,0:T(8,128)} %get-tuple-element.20) | copy-start | bytes 1572868
where the time goes:
time: 98.6 us; the launch traced here: 98 us
  blocking collectives  54.1 us (55%)
  Pallas kernels  29.6 us (30%)
  starting transfers between devices  7.41 us (8%)
  local copies, waits for them, and re-layouts  5.38 us (5%)
    all_to_all x4, blocking collectives, exchange(): return lax.all_to_all(x, axes, split_axis=0, concat_axis=0, tiled=True)  54.1 us
    pallas_call x1, Pallas kernels, per_device(): call(solve_kernel, (struct(groups, 4, h_dev, BS), struct(4, 2, BS, BS, dt...  12.8 us
    all_to_all x1, starting transfers between devices, exchange(): return lax.all_to_all(x, axes, split_axis=0, concat_axis=0, tiled=True)  7.41 us
    pallas_call x1, Pallas kernels, per_device(): call(image_kernel, (struct(2, h_dev, nodes_dev), struct(world, LANES)), [...  5.27 us
    pallas_call x1, Pallas kernels, per_device(): call(prep_kernel, (struct(blk, BS, BS), struct(1, LANES)), [VMEM, VMEM],...  4.32 us
    unnamed x8, local copies, waits for them, and re-layouts  3.39 us
    pallas_call x1, Pallas kernels, per_device(): call(column_kernel, struct(harm, 2, h_dev, BS), [SMEM] + [VMEM] * 7, VMEM...  3.22 us
    pallas_call x1, Pallas kernels, per_device(): call(lambda *refs: rest_kernel(count, *refs), (struct(2, h_dev, nodes_dev...  2.27 us
  transfers between devices with their start and end apart: 1, of which 1 were waited for; matrix products, arithmetic and copies ran while one was open for 2% of the time, Pallas kernels for 4%

commit v1 on v0

v1 whole, which is shorter than its diff:
```python
import math

import jax
import jax.numpy as jnp
import numpy as np
from jax import lax
from jax.experimental import pallas as pl
from jax.experimental.pallas import tpu as pltpu
from jax.sharding import Mesh
from jax.sharding import PartitionSpec as P

BS = 256
H = 64
NEIGH = 2
KRY = 8
HARM = ("harm_0", "harm_1")
NODE = ("node_0", "node_1")
NODE_HARM = ("node_0", "node_1", "harm_0", "harm_1")
F32 = jnp.float32
BF16 = jnp.bfloat16
LANES = 128
GRAM = 64
SMEM = pl.BlockSpec(memory_space=pltpu.SMEM)
VMEM = pl.BlockSpec(memory_space=pltpu.VMEM)
ANY = pl.BlockSpec(memory_space=pl.ANY)


def spectral_tables():
    steps = np.arange(H)
    angles = (steps[:, None] * steps[None, :] % H) * (2.0 * math.pi / H)
    cosine = np.cos(angles) / math.sqrt(H)
    sine = np.sin(angles) / math.sqrt(H)
    table = np.block([[cosine, -sine], [sine, cosine]]).astype(np.float32)
    both = np.stack([table, table.T])
    high = both.astype(jnp.bfloat16)
    low = (both - high.astype(np.float32)).astype(jnp.bfloat16)
    return high, low


def split(x):
    high = x.astype(BF16)
    return high, (x - high.astype(F32)).astype(BF16)


def mm(a, b):
    return jnp.dot(a, b, preferred_element_type=F32)


def mm_t(a, b):
    return lax.dot_general(a, b, (((1,), (1,)), ((), ())), preferred_element_type=F32)


def rows_mm(x, w_high, w_low, product=mm):
    rows = x.shape[0]
    high, low = split(x)
    both = product(jnp.concatenate([high, low], axis=0), w_high)
    return both[:rows] + both[rows:] + product(high, w_low)


def sublane_sum(x):
    return jnp.sum(x, axis=0, keepdims=True)


def rows_to_lanes(rows):
    return sublane_sum(jnp.transpose(rows))


def index_kernel(nb_ref, pat_ref, hot_ref):
    groups = hot_ref.shape[0]
    blk = nb_ref.shape[1]
    for q in range(groups):
        hot_ref[q, 0] = blk
        hot_ref[q, 1] = -1
    for b in range(blk):
        for j in range(NEIGH):
            block = nb_ref[j, b]
            group = block // blk
            local = block - group * blk

            @pl.when(pat_ref[j, b] > 0)
            def _():
                hot_ref[group, 0] = jnp.minimum(hot_ref[group, 0], local)
                hot_ref[group, 1] = jnp.maximum(hot_ref[group, 1], local)


def pack_kernel(k_ref, cond_ref, out_ref, held, sem):
    copy = pltpu.make_async_copy(k_ref.at[KRY - 1], held, sem)
    copy.start()
    blk = out_ref.shape[0]
    sums = jnp.concatenate(
        [sublane_sum(cond_ref[:, BS * b : BS * (b + 1)]) for b in range(blk)], axis=0
    )
    for b in range(blk):
        out_ref[b, 2] = cond_ref[:, BS * b : BS * (b + 1)]
        out_ref[b, 3] = sums
    copy.wait()
    for b in range(blk):
        cols = slice(BS * b, BS * (b + 1))
        out_ref[b, 0] = held[0, :, cols]
        out_ref[b, 1] = held[1, :, cols]


def turn_kernel(diag_ref, t_ref, held, sems):
    blk = t_ref.shape[0]
    copies = [pltpu.make_async_copy(diag_ref.at[b], held.at[b], sems.at[b]) for b in range(blk)]
    for copy in copies:
        copy.start()
    for b, copy in enumerate(copies):
        copy.wait()
        t_ref[b] = jnp.transpose(held[b])


def gram_kernel(k_ref, gram_ref, rows):
    rows[...] = jnp.zeros_like(rows)
    chunks = k_ref.shape[3] // LANES
    for m in range(KRY):
        real = [None] * KRY
        imag = [None] * KRY
        for c in range(chunks):
            cols = slice(LANES * c, LANES * (c + 1))
            mr, mi = k_ref[m, 0, :, cols], k_ref[m, 1, :, cols]
            for n in range(m, KRY):
                nr, ni = (mr, mi) if n == m else (k_ref[n, 0, :, cols], k_ref[n, 1, :, cols])
                r = mr * nr + mi * ni
                real[n] = r if c == 0 else real[n] + r
                if n > m:
                    i = mr * ni - mi * nr
                    imag[n] = i if c == 0 else imag[n] + i
        for n in range(m, KRY):
            at = GRAM + KRY * m + n
            rows[at : at + 1] = sublane_sum(real[n])
            if n > m:
                at = GRAM + KRY * n + m
                rows[at : at + 1] = sublane_sum(imag[n])
    gram_ref[...] = rows_to_lanes(rows[...])


def powers_of(e_ref, b, at, turned, d):
    e_ref[b, at, 0], e_ref[b, at, 1] = split(turned * (-d))


def squared_with(e_ref, u_ref, b, p):
    high, low = e_ref[b, p, 0], e_ref[b, p, 1]
    u = u_ref[b]
    rows = u.shape[0]
    u_high, u_low = split(u)
    x = mm(jnp.concatenate([high, low, u_high, u_low], axis=0), high)
    y = mm(jnp.concatenate([high, u_high], axis=0), low)
    u_ref[b] = u + (x[2 * BS : 2 * BS + rows] + x[2 * BS + rows :] + y[BS:])
    e_ref[b, p + 1, 0], e_ref[b, p + 1, 1] = split(x[:BS] + x[BS : 2 * BS] + y[:BS])


def solve_kernel(got_ref, t_ref, k_ref, means_ref, u_ref, e_ref, d_ref):
    blk = t_ref.shape[0]
    powers = e_ref.shape[1]
    means = got_ref[0, 3]
    for s in range(1, got_ref.shape[0]):
        means = means + got_ref[s, 3]
    means = means * (1.0 / H)
    means_ref[...] = means
    d_ref[...] = 1.0 / means
    for b in range(blk):
        d = d_ref[b : b + 1]
        powers_of(e_ref, b, 0, t_ref[b], d)
        cols = slice(b * BS, (b + 1) * BS)
        u_ref[b] = jnp.concatenate([k_ref[KRY - 1, 0, :, cols], k_ref[KRY - 1, 1, :, cols]], axis=0) * d

    def stage(p, carry):
        for b in range(blk):
            squared_with(e_ref, u_ref, b, p)
        return carry

    lax.fori_loop(0, powers - 1, stage, 0)
    for b in range(blk):
        u = u_ref[b]
        u_ref[b] = u + rows_mm(u, e_ref[b, powers - 1, 0], e_ref[b, powers - 1, 1])
    for b in range(blk):
        u = u_ref[b]
        twice = rows_mm(u, e_ref[b, powers - 1, 0], e_ref[b, powers - 1, 1])
        u_ref[b] = u + rows_mm(twice, e_ref[b, powers - 1, 0], e_ref[b, powers - 1, 1])


def select_kernel(hot_ref, u_ref, send_ref, sems):
    blk = u_ref.shape[0]
    groups = send_ref.shape[0]
    me = lax.axis_index(NODE)
    for wait in (False, True):
        for at, offset in enumerate((1, 2, 3, -1, -2, -3)):
            group = me + offset

            @pl.when((group >= 0) & (group < groups))
            def _():
                first = jnp.minimum(hot_ref[group, 0], blk - 1)
                second = jnp.maximum(hot_ref[group, 1], 0)
                for slot, b in enumerate((first, second)):
                    copy = pltpu.make_async_copy(u_ref.at[b], send_ref.at[group, slot], sems.at[at, slot])
                    if wait:
                        copy.wait()
                    else:
                        copy.start()


def column_kernel(got_ref, diag_ref, means_ref, cap_ref, high_ref, low_ref, out_ref, held, sem, u_ref, e_ref):
    own = lax.axis_index(HARM)
    copy = pltpu.make_async_copy(diag_ref.at[own], held, sem)
    copy.start()
    sources = got_ref.shape[0]
    powers = e_ref.shape[1]
    mean = means_ref[pl.ds(own, 1), :]
    d = 1.0 / mean
    u_ref[0] = jnp.concatenate([got_ref[s, p] for p in range(2) for s in range(sources)], axis=0) * d
    copy.wait()
    powers_of(e_ref, 0, 0, jnp.transpose(held[...]), d)
    for p in range(powers - 1):
        squared_with(e_ref, u_ref, 0, p)
    u = u_ref[0]
    u = u + rows_mm(u, e_ref[0, powers - 1, 0], e_ref[0, powers - 1, 1])
    twice = rows_mm(u, e_ref[0, powers - 1, 0], e_ref[0, powers - 1, 1])
    u = u + rows_mm(twice, e_ref[0, powers - 1, 0], e_ref[0, powers - 1, 1])
    direct = rows_mm(u, e_ref[0, 0, 0], e_ref[0, 0, 1]) * (-mean)

    def transform(way, x):
        high, low = split(x)
        table = high_ref[way]
        return mm(table, high) + mm(table, low) + mm(low_ref[way], high)

    cond = jnp.concatenate([got_ref[s, 2] for s in range(sources)], axis=0)
    driven = transform(0, u) * jnp.concatenate([cond, cond], axis=0)
    image = direct + transform(1, driven)
    cap = cap_ref[pl.ds(pl.multiple_of(own * BS, BS), BS)].reshape(1, BS)
    harmonic = lax.broadcasted_iota(jnp.int32, (H, BS), 0)
    omega = jnp.where(harmonic < H // 2, harmonic, harmonic - H)
    react = omega.astype(F32) * cap
    real = image[:H] - react * u[H:]
    imag = image[H:] + react * u[:H]
    step = H // sources
    for s in range(sources):
        out_ref[s, 0] = real[step * s : step * (s + 1)]
        out_ref[s, 1] = imag[step * s : step * (s + 1)]


def couple_kernel(nb_ref, pat_ref, hot_ref, got_ref, c_ref, out_ref, held, sems):
    blk = held.shape[0]
    half = out_ref.shape[1]
    copies = [pltpu.make_async_copy(c_ref.at[b], held.at[b], sems.at[b]) for b in range(blk)]
    for copy in copies:
        copy.start()
    for b, copy in enumerate(copies):
        copy.wait()
        total = None
        for j in range(NEIGH):
            block = nb_ref[j, b]
            group = block // blk
            second = jnp.where(block - group * blk == hot_ref[group, 0], 0, 1)
            x = jnp.where(pat_ref[j, b] > 0, got_ref[group, second], 0.0)
            term = rows_mm(x, *split(held[b, j]), product=mm_t)
            total = term if j == 0 else total + term
        cols = slice(b * BS, (b + 1) * BS)
        out_ref[0, :, cols] = total[:half]
        out_ref[1, :, cols] = total[half:]


def image_kernel(back_ref, coupled_ref, k_ref, gram_ref, image_ref, send_ref, rows):
    chunks = k_ref.shape[3] // LANES
    real = [None] * KRY
    imag = [None] * KRY
    squares = None
    for c in range(chunks):
        cols = slice(LANES * c, LANES * (c + 1))
        block, at = LANES * c // BS, LANES * c % BS
        ir = coupled_ref[0, :, cols] + back_ref[block, 0, :, at : at + LANES]
        ii = coupled_ref[1, :, cols] + back_ref[block, 1, :, at : at + LANES]
        image_ref[0, :, cols] = ir
        image_ref[1, :, cols] = ii
        both = ir * ir + ii * ii
        squares = both if c == 0 else squares + both
        for m in range(KRY):
            mr, mi = k_ref[m, 0, :, cols], k_ref[m, 1, :, cols]
            r = mr * ir + mi * ii
            i = mr * ii - mi * ir
            real[m] = r if c == 0 else real[m] + r
            imag[m] = i if c == 0 else imag[m] + i
    rows[...] = jnp.zeros_like(rows)
    for m in range(KRY):
        rows[m : m + 1] = sublane_sum(real[m])
        rows[KRY + m : KRY + m + 1] = sublane_sum(imag[m])
    rows[2 * KRY : 2 * KRY + 1] = sublane_sum(squares)
    row = rows_to_lanes(rows[...]) + gram_ref[...]
    send_ref[...] = jnp.broadcast_to(row, send_ref.shape)


def rest_kernel(count, got_ref, image_ref, k_ref, vector_ref, proj_ref, norm_ref):
    totals = sublane_sum(got_ref[...]) * (1.0 / count)
    lane = lax.broadcasted_iota(jnp.int32, totals.shape, 1)

    def at(q):
        return jnp.broadcast_to(totals[:, q : q + 1], totals.shape)

    pr = [at(m) for m in range(KRY)]
    pi = [at(KRY + m) for m in range(KRY)]
    row_r = row_i = col_r = col_i = jnp.zeros_like(totals)
    row_of = (lane - GRAM) // KRY
    col_of = (lane - GRAM) - row_of * KRY
    for m in range(KRY):
        row_r = jnp.where(row_of == m, pr[m], row_r)
        row_i = jnp.where(row_of == m, pi[m], row_i)
        col_r = jnp.where(col_of == m, pr[m], col_r)
        col_i = jnp.where(col_of == m, pi[m], col_i)
    upper = row_r * col_r + row_i * col_i
    lower = col_i * row_r - col_r * row_i
    weight = jnp.where(row_of == col_of, upper, 2.0 * jnp.where(row_of < col_of, upper, lower))
    weight = jnp.where(lane >= GRAM, weight, 0.0)
    weight = jnp.where(lane < 2 * KRY, -2.0 * totals, weight)
    weight = jnp.where(lane == 2 * KRY, 1.0, weight)
    squares = jnp.sum(totals * weight, axis=1, keepdims=True)
    norm = jnp.sqrt(squares + 1e-06)
    norm_ref[...] = norm
    for m in range(KRY):
        proj_ref[0:1, m : m + 1] = pr[m][:, 0:1]
        proj_ref[1:2, m : m + 1] = pi[m][:, 0:1]
    half = k_ref.shape[2]
    scale = jnp.broadcast_to(1.0 / norm, (half, LANES))
    pr = [jnp.broadcast_to(x, (half, LANES)) for x in pr]
    pi = [jnp.broadcast_to(x, (half, LANES)) for x in pi]
    for c in range(k_ref.shape[3] // LANES):
        cols = slice(LANES * c, LANES * (c + 1))
        real, imag = image_ref[0, :, cols], image_ref[1, :, cols]
        for m in range(KRY):
            mr, mi = k_ref[m, 0, :, cols], k_ref[m, 1, :, cols]
            real = real - (pr[m] * mr - pi[m] * mi)
            imag = imag - (pr[m] * mi + pi[m] * mr)
        vector_ref[0, :, cols] = real * scale
        vector_ref[1, :, cols] = imag * scale


def struct(*dims, dtype=F32):
    return pltpu.VMEM(dims, dtype)


def far(*dims, dtype=F32):
    return jax.ShapeDtypeStruct(dims, dtype)


def near(x):
    return pltpu.with_memory_space_constraint(x, pltpu.VMEM)


def call(kernel, out_shape, in_specs, flops, scratch=(), out_specs=None):
    single = not isinstance(out_shape, tuple)
    return pl.pallas_call(
        kernel,
        out_shape=out_shape,
        in_specs=in_specs,
        out_specs=out_specs or (VMEM if single else (VMEM,) * len(out_shape)),
        scratch_shapes=list(scratch),
        cost_estimate=pl.CostEstimate(flops=flops, bytes_accessed=1 << 20, transcendentals=0),
    )


def exchange(x, axes):
    return lax.all_to_all(x, axes, split_axis=0, concat_axis=0, tiled=True)


def per_device(krylov_basis, cond_time, capacity, diag_blocks, coupling, neighbours, pattern):
    h_dev = krylov_basis.shape[2]
    nodes_dev = krylov_basis.shape[3]
    blk = diag_blocks.shape[0]
    harm = lax.axis_size(HARM)
    groups = lax.axis_size(NODE)
    world = groups * harm
    names, present = neighbours.T, pattern.T
    krylov = near(krylov_basis)
    lanes = [pltpu.VMEM((LANES, LANES), F32)]

    packed = call(
        pack_kernel,
        far(blk, 4, h_dev, BS),
        [ANY, VMEM],
        1 << 20,
        [pltpu.VMEM((2, h_dev, nodes_dev), F32), pltpu.SemaphoreType.DMA],
    )(krylov_basis, cond_time)
    got = near(exchange(packed, HARM))
    hot_own = call(
        index_kernel, far(groups, LANES, dtype=jnp.int32), [SMEM, SMEM], 1 << 10, out_specs=SMEM
    )(names, present)
    hot = exchange(hot_own, NODE)
    turned = call(
        turn_kernel,
        struct(blk, BS, BS),
        [ANY],
        1 << 24,
        [pltpu.VMEM((blk, BS, BS), F32), pltpu.SemaphoreType.DMA((blk,))],
    )(diag_blocks)
    gram = call(gram_kernel, far(1, LANES), [VMEM], 1 << 24, lanes)(krylov)
    powers = 3
    means, solved = call(
        solve_kernel,
        (far(blk, BS), struct(blk, 2 * h_dev, BS)),
        [VMEM] * 3,
        1 << 31,
        [pltpu.VMEM((blk, powers, 2, BS, BS), BF16), pltpu.VMEM((blk, BS), F32)],
    )(got, near(turned), krylov)
    send_hot = call(
        select_kernel,
        far(groups, 2, 2 * h_dev, BS),
        [SMEM, VMEM],
        1 << 10,
        [pltpu.SemaphoreType.DMA((6, 2))],
        out_specs=ANY,
    )(hot, near(solved))
    named = near(exchange(send_hot, NODE))
    high, low = spectral_tables()
    send_cols = call(
        column_kernel,
        far(harm, 2, h_dev, BS),
        [VMEM, ANY] + [VMEM] * 4,
        1 << 27,
        [
            pltpu.VMEM((BS, BS), F32),
            pltpu.SemaphoreType.DMA,
            pltpu.VMEM((1, 2 * H, BS), F32),
            pltpu.VMEM((1, powers, 2, BS, BS), BF16),
        ],
    )(got, diag_blocks, means, capacity, jnp.asarray(high), jnp.asarray(low))
    back = near(exchange(send_cols, HARM))
    coupled = call(
        couple_kernel,
        struct(2, h_dev, nodes_dev),
        [SMEM] * 3 + [VMEM, ANY],
        1 << 28,
        [pltpu.VMEM(coupling.shape, F32), pltpu.SemaphoreType.DMA((blk,))],
    )(names, present, hot_own, named, coupling)
    image, send_sums = call(
        image_kernel,
        (struct(2, h_dev, nodes_dev), struct(world, LANES)),
        [VMEM] * 4,
        1 << 24,
        lanes,
    )(back, near(coupled), krylov, gram)
    sums = near(exchange(send_sums, NODE_HARM))
    count = world * h_dev * nodes_dev
    vector, proj, norm = call(
        lambda *refs: rest_kernel(count, *refs),
        (far(2, h_dev, nodes_dev), far(2, KRY), far(1, 1)),
        [VMEM] * 3,
        1 << 24,
    )(sums, near(image), krylov)
    return vector, proj, norm.reshape(())


def solution(mesh):
    finer = Mesh(mesh.devices.reshape(4, 4, 4, 2), ("node_0", "node_1", "harm_0", "harm_1"))
    placed = (
        P(None, None, HARM, NODE),
        P(HARM, NODE),
        P(NODE),
        P(NODE, None, None),
        P(NODE, None, None, None),
        P(NODE, None),
        P(NODE, None),
    )

    return jax.shard_map(
        per_device,
        mesh=finer,
        in_specs=placed,
        out_specs=(P(None, HARM, NODE), P(), P()),
        check_vma=False,
    )
```

time: 98.6 us -> 78.4 us (0.80)
  blocking collectives: 54.1 us -> 14.8 us
  starting transfers between devices: 7.41 us -> 25.7 us
  waiting for transfers between devices: 0.23 us -> 8.81 us
  Pallas kernels: 29.6 us -> 24 us
  local copies, waits for them, and re-layouts: 5.38 us -> 3.47 us
    all_to_all x4 -> x1, blocking collectives: 54.1 us -> 14.8 us  [exchange(): return lax.all_to_all(x, axes, split_axis=0, concat_axis=0, tiled=True)]
    all_to_all x1 -> x4, starting transfers between devices: 7.41 us -> 25.7 us  [exchange(): return lax.all_to_all(x, axes, split_axis=0, concat_axis=0, tiled=True)]
    all_to_all x1 -> x4, waiting for transfers between devices: 0.23 us -> 8.81 us  [exchange(): return lax.all_to_all(x, axes, split_axis=0, concat_axis=0, tiled=True)]
    pallas_call x1, Pallas kernels: 5.27 us -> 0.95 us  [per_device(): call(image_kernel, (struct(2, h_dev, nodes_dev), struct(world, LANES)), [...]
    reshape x1 -> x0, local copies, waits for them, and re-layouts: 1.3 us -> none  [per_device(): capacity.reshape(blk, BS)]
    pallas_call x5 -> x9, Pallas kernels: 24.3 us -> 23.1 us  [the longest x1 5.03 us: per_device(): call(couple_kernel, struct(2, h_dev, nodes_dev), [SMEM] * 3 + [VMEM, ANY]...]
    unnamed x8 -> x10, local copies, waits for them, and re-layouts: 3.39 us -> 3.47 us
  transfers between devices with their start and end apart: 1 -> 4, of which waited for: 1 -> 3; matrix products, arithmetic and copies ran while one was open for 2% -> 0% of each run, Pallas kernels for 4% -> 23%
where the time goes in v1:
time: 78.4 us; the launch traced here: 77.6 us
  starting transfers between devices  25.7 us (33%)
  Pallas kernels  24 us (31%)
  blocking collectives  14.8 us (19%)
  waiting for transfers between devices  8.81 us (11%)
  local copies, waits for them, and re-layouts  3.47 us (4%)
    all_to_all x4, starting transfers between devices, exchange(): return lax.all_to_all(x, axes, split_axis=0, concat_axis=0, tiled=True)  25.7 us
    all_to_all x1, blocking collectives, exchange(): return lax.all_to_all(x, axes, split_axis=0, concat_axis=0, tiled=True)  14.8 us
    all_to_all x4, waiting for transfers between devices, exchange(): return lax.all_to_all(x, axes, split_axis=0, concat_axis=0, tiled=True)  8.81 us
    pallas_call x1, Pallas kernels, per_device(): call(couple_kernel, struct(2, h_dev, nodes_dev), [SMEM] * 3 + [VMEM, ANY]...  5.03 us
    pallas_call x1, Pallas kernels, per_device(): call(column_kernel, far(harm, 2, h_dev, BS), [VMEM, ANY] + [VMEM] * 4, 1...  4.49 us
    pallas_call x1, Pallas kernels, per_device(): call(solve_kernel, (far(blk, BS), struct(blk, 2 * h_dev, BS)), [VMEM] * 3...  3.71 us
    unnamed x10, local copies, waits for them, and re-layouts  3.47 us
    pallas_call x1, Pallas kernels, per_device(): call(pack_kernel, far(blk, 4, h_dev, BS), [ANY, VMEM], 1 << 20, [pltpu.VM...  2.46 us
  transfers between devices with their start and end apart: 4, of which 3 were waited for; matrix products, arithmetic and copies ran while one was open for 0% of the time, Pallas kernels for 23%

profile of v1, /device:TPU:1, one launch (start us, length us, event | category | flops | bytes accessed | tf_op | source)
XLA Modules:
  0.0 77.6 jit_solution(4540092611402417298)
XLA Ops:
  0.6 2.5 %shard_map.112 = f32[8,4,8,256]{3,2,1,0:T(8,128)} custom-call(f32[8,2,8,2048]{3,2,1,0:T(8,128)} %refs_2_.1, f32[8,2048]{1,0:T(8,128)} %cond_ref.1), custom_call_target="tpu_custom_call" | custom-call | flops 1048576 | bytes 1048576 | tf_op jit(solution)/shard_map/pallas_call | solution.py:375
  3.1 6.8 %all-to-all-start = ((f32[8,4,8,256]{3,2,1,0:T(8,128)}), f32[8,4,8,256]{3,2,1,0:T(8,128)S(1)}, u32[]{:S(2)}, u32[]{:S(2)}) async-start(f32[8,4,8,256]{3,2,1,0:T(8,128)} %shard_map.112), calls=%async_computation | async-start | bytes 524288 | tf_op jit(solution)/shard_map/all_to_all | solution.py:361
  9.9 1.5 %shard_map.116.hot_ref = s32[16,128]{1,0:T(8,128)} custom-call(s32[2,8]{1,0:T(2,128)} %bitcast.14, s32[2,8]{1,0:T(2,128)} %bitcast.16), custom_call_target="tpu_custom_call" | custom-call | flops 1024 | bytes 1048576 | tf_op jit(solution)/shard_map/pallas_call | solution.py:383
  11.5 2.1 %shard_map.113.t_ref = f32[8,256,256]{2,1,0:T(8,128)S(1)} custom-call(f32[8,256,256]{2,1,0:T(8,128)} %diag_ref.3), custom_call_target="tpu_custom_call" | custom-call | flops 16777216 | bytes 1048576 | tf_op jit(solution)/shard_map/pallas_call | solution.py:387
  13.6 2.8 %all-to-all-done.got_ref = f32[8,4,8,256]{3,2,1,0:T(8,128)S(1)} async-done(((f32[8,4,8,256]{3,2,1,0:T(8,128)}), f32[8,4,8,256]{3,2,1,0:T(8,128)S(1)}, u32[]{:S(2)}, u32[]{:S(2)}) %all-to-all-start) | async-done | bytes 262176 | tf_op jit(solution)/shard_map/all_to_all | solution.py:361
  16.4 0.0 copy-start.2
  16.4 0.7 copy-done.2
  17.1 6.8 %all-to-all-start.2 = ((s32[16,1,128]{2,1,0:T(1,128)}), s32[16,1,128]{2,1,0:T(1,128)S(1)}, u32[]{:S(2)}, u32[]{:S(2)}) async-start(s32[16,1,128]{2,1,0:T(1,128)} %bitcast.3), calls=%async_computation.2 | async-start | bytes 16384 | tf_op jit(solution)/shard_map/all_to_all | solution.py:361
  23.8 0.0 copy-start
  23.9 1.2 %copy-done = f32[8,2,8,2048]{3,2,1,0:T(8,128)S(1)} copy-done((f32[8,2,8,2048]{3,2,1,0:T(8,128)S(1)}, f32[8,2,8,2048]{3,2,1,0:T(8,128)}, u32[]{:S(2)}) %copy-start) | copy-done | bytes 1048600
  25.1 0.0 copy-start.3
  25.1 0.9 %copy-done.3 = f32[8,4,8,256]{3,2,1,0:T(8,128)S(1)} copy-done((f32[8,4,8,256]{3,2,1,0:T(8,128)S(1)}, f32[8,4,8,256]{3,2,1,0:T(8,128)}, u32[]{:S(2)}) %copy-start.3) | copy-done | bytes 262168
  26.0 3.7 %shard_map.114 = (f32[8,256]{1,0:T(8,128)}, f32[8,16,256]{2,1,0:T(8,128)S(1)}) custom-call(f32[8,4,8,256]{3,2,1,0:T(8,128)S(1)} %copy-done.3, f32[8,256,256]{2,1,0:T(8,128)S(1)} %shard_map.113.t_ref, f32[8,2,8,2048]{3,2,1,0:T(8,128)S(1)} %copy-done), custom_call_target="tpu_custom_call" | custom-call | flops 2147483648 | bytes 1048576 | tf_op jit(solution)/shard_map/pallas_call | solution.py:396
  29.7 0.6 all-to-all-done.2
  30.3 0.0 copy-start.4
  30.3 0.6 copy-done.4
  30.9 1.6 %shard_map.117 = f32[16,2,16,256]{3,2,1,0:T(8,128)} custom-call(s32[16,128]{1,0:T(8,128)} %bitcast.13, f32[8,16,256]{2,1,0:T(8,128)S(1)} %get-tuple-element.11.u_ref), custom_call_target="tpu_custom_call" | custom-call | flops 1024 | bytes 1048576 | tf_op jit(solution)/shard_map/pallas_call | solution.py:403
  32.5 0.0 copy-start.1
  32.5 6.3 %all-to-all-start.3 = ((f32[16,2,16,256]{3,2,1,0:T(8,128)}), f32[16,2,16,256]{3,2,1,0:T(8,128)S(1)}, u32[]{:S(2)}, u32[]{:S(2)}) async-start(f32[16,2,16,256]{3,2,1,0:T(8,128)} %shard_map.117), calls=%async_computation.3 | async-start | bytes 1048576 | tf_op jit(solution)/shard_map/all_to_all | solution.py:361
  38.8 4.5 %shard_map.115 = f32[8,2,8,256]{3,2,1,0:T(8,128)} custom-call(f32[8,4,8,256]{3,2,1,0:T(8,128)S(1)} %copy-done.3, f32[8,256,256]{2,1,0:T(8,128)} %diag_ref.3, f32[8,256]{1,0:T(8,128)} %get-tuple-element.10.means_ref, f32[2048]{0:T(1024)} %cap_ref.1, bf16[2,128,128]{2,1,0:T(8,128)(2,1)} %constant.4.clone.high_ref, bf16[2,128,128]{2,1,0:T(8,128)(2,1)} %constant.5.clone.low_ref), custom_call_target="tpu_custom_call" | custom-call | flops 134217728 | bytes 1048576 | tf_op jit(solution)/shard_map/pallas_call | solution.py:413
  43.3 5.4 %all-to-all-done.3.got_ref = f32[16,2,16,256]{3,2,1,0:T(8,128)S(1)} async-done(((f32[16,2,16,256]{3,2,1,0:T(8,128)}), f32[16,2,16,256]{3,2,1,0:T(8,128)S(1)}, u32[]{:S(2)}, u32[]{:S(2)}) %all-to-all-start.3) | async-done | bytes 524320 | tf_op jit(solution)/shard_map/all_to_all | solution.py:361
  48.7 5.9 %all-to-all-start.1 = ((f32[8,2,8,256]{3,2,1,0:T(8,128)}), f32[8,2,8,256]{3,2,1,0:T(8,128)S(1)}, u32[]{:S(2)}, u32[]{:S(2)}) async-start(f32[8,2,8,256]{3,2,1,0:T(8,128)} %shard_map.115), calls=%async_computation.1 | async-start | bytes 262144 | tf_op jit(solution)/shard_map/all_to_all | solution.py:361
  54.6 0.0 copy-done.1
  54.6 1.2 %shard_map.119.gram_ref = f32[1,128]{1,0:T(1,128)} custom-call(f32[8,2,8,2048]{3,2,1,0:T(8,128)S(1)} %copy-done.1), custom_call_target="tpu_custom_call" | custom-call | flops 16777216 | bytes 1048576 | tf_op jit(solution)/shard_map/pallas_call | solution.py:394
  55.8 5.0 %shard_map.118.coupled_ref = f32[2,8,2048]{2,1,0:T(8,128)S(1)} custom-call(s32[2,8]{1,0:T(2,128)} %bitcast.15, s32[2,8]{1,0:T(2,128)} %bitcast.17, s32[16,128]{1,0:T(8,128)} %shard_map.116.hot_ref, f32[16,2,16,256]{3,2,1,0:T(8,128)S(1)} %all-to-all-done.3.got_ref, f32[8,2,256,256]{3,2,1,0:T(8,128)} %c_ref.1), custom_call_target="tpu_custom_call" | custom-call | flops 268435456 | bytes 1048576 | tf_op jit(solution)/shard_map/pallas_call | solution.py:426
  60.8 0.0 all-to-all-done.1.back_ref
  60.8 0.9 %shard_map.120 = (f32[2,8,2048]{2,1,0:T(8,128)S(1)}, f32[128,128]{1,0:T(8,128)S(1)}) custom-call(f32[8,2,8,256]{3,2,1,0:T(8,128)S(1)} %all-to-all-done.1.back_ref, f32[2,8,2048]{2,1,0:T(8,128)S(1)} %shard_map.118.coupled_ref, f32[8,2,8,2048]{3,2,1,0:T(8,128)S(1)} %copy-done.1, f32[1,128]{1,0:T(1,128)} %shard_map.119.gram_ref), custom_call_target="tpu_custom_call" | custom-call | flops 16777216 | bytes 1048576 | tf_op jit(solution)/shard_map/pallas_call | solution.py:433
  61.8 14.8 %all_to_all.37 = f32[128,1,128]{2,1,0:T(1,128)S(1)} all-to-all(f32[128,1,128]{2,1,0:T(1,128)S(1)} %bitcast.12), channel_id=1, replica_groups=mesh['node_0'=4,'node_1'=4,'harm_0'=4,'harm_1'=2] {'node_0','node_1','ha..., dimensions={0} | all-to-all | bytes 131072 | tf_op jit(solution)/shard_map/all_to_all | solution.py:361
  76.6 1.0 %shard_map.121 = (f32[2,8,2048]{2,1,0:T(8,128)}, f32[2,8]{1,0:T(2,128)}, f32[1,1]{1,0:T(1,128)}) custom-call(f32[128,128]{1,0:T(8,128)S(1)} %bitcast.11, f32[2,8,2048]{2,1,0:T(8,128)S(1)} %get-tuple-element.13.refs_1_, f32[8,2,8,2048]{3,2,1,0:T(8,128)S(1)} %copy-done.1), custom_call_target="tpu_custom_call" | custom-call | flops 16777216 | bytes 1048576 | tf_op jit(solution)/shard_map/pallas_call | solution.py:442
Async XLA Ops:
  3.1 13.3 %all-to-all-start = ((f32[8,4,8,256]{3,2,1,0:T(8,128)}), f32[8,4,8,256]{3,2,1,0:T(8,128)S(1)}, u32[]{:S(2)}, u32[]{:S(2)}) async-start(f32[8,4,8,256]{3,2,1,0:T(8,128)} %shard_map.112), calls=%async_computation | async-start | bytes 524288 | tf_op jit(solution)/shard_map/all_to_all | solution.py:361
  16.4 0.7 copy-start.2
  17.1 13.2 %all-to-all-start.2 = ((s32[16,1,128]{2,1,0:T(1,128)}), s32[16,1,128]{2,1,0:T(1,128)S(1)}, u32[]{:S(2)}, u32[]{:S(2)}) async-start(s32[16,1,128]{2,1,0:T(1,128)} %bitcast.3), calls=%async_computation.2 | async-start | bytes 16384 | tf_op jit(solution)/shard_map/all_to_all | solution.py:361
  23.8 1.2 %copy-start = (f32[8,2,8,2048]{3,2,1,0:T(8,128)S(1)}, f32[8,2,8,2048]{3,2,1,0:T(8,128)}, u32[]{:S(2)}) copy-start(f32[8,2,8,2048]{3,2,1,0:T(8,128)} %refs_2_.1) | copy-start | bytes 3145732
  25.1 0.9 %copy-start.3 = (f32[8,4,8,256]{3,2,1,0:T(8,128)S(1)}, f32[8,4,8,256]{3,2,1,0:T(8,128)}, u32[]{:S(2)}) copy-start(f32[8,4,8,256]{3,2,1,0:T(8,128)} %copy-done.2) | copy-start | bytes 786436
  30.3 0.6 copy-start.4
  32.5 22.1 %copy-start.1 = (f32[8,2,8,2048]{3,2,1,0:T(8,128)S(1)}, f32[8,2,8,2048]{3,2,1,0:T(8,128)}, u32[]{:S(2)}) copy-start(f32[8,2,8,2048]{3,2,1,0:T(8,128)} %refs_2_.1) | copy-start | bytes 3145732
  32.5 16.2 %all-to-all-start.3 = ((f32[16,2,16,256]{3,2,1,0:T(8,128)}), f32[16,2,16,256]{3,2,1,0:T(8,128)S(1)}, u32[]{:S(2)}, u32[]{:S(2)}) async-start(f32[16,2,16,256]{3,2,1,0:T(8,128)} %shard_map.117), calls=%async_computation.3 | async-start | bytes 1048576 | tf_op jit(solution)/shard_map/all_to_all | solution.py:361
  48.7 12.1 %all-to-all-start.1 = ((f32[8,2,8,256]{3,2,1,0:T(8,128)}), f32[8,2,8,256]{3,2,1,0:T(8,128)S(1)}, u32[]{:S(2)}, u32[]{:S(2)}) async-start(f32[8,2,8,256]{3,2,1,0:T(8,128)} %shard_map.115), calls=%async_computation.1 | async-start | bytes 262144 | tf_op jit(solution)/shard_map/all_to_all | solution.py:361

commit v2 on v0

v2 whole, which is shorter than its diff:
```python
import math

import jax
import jax.numpy as jnp
import numpy as np
from jax import lax
from jax.experimental import pallas as pl
from jax.experimental.pallas import tpu as pltpu
from jax.sharding import Mesh
from jax.sharding import PartitionSpec as P

BS = 256
H = 64
NEIGH = 2
KRY = 8
HARM = ("harm_0", "harm_1")
NODE = ("node_0", "node_1")
NODE_HARM = ("node_0", "node_1", "harm_0", "harm_1")
F32 = jnp.float32
BF16 = jnp.bfloat16
LANES = 128
CODE = 16
OFFSETS = (1, 2, 3, -1, -2, -3)
GRAM = 64
SMEM = pl.BlockSpec(memory_space=pltpu.SMEM)
VMEM = pl.BlockSpec(memory_space=pltpu.VMEM)
ANY = pl.BlockSpec(memory_space=pl.ANY)


def spectral_tables():
    steps = np.arange(H)
    angles = (steps[:, None] * steps[None, :] % H) * (2.0 * math.pi / H)
    cosine = np.cos(angles) / math.sqrt(H)
    sine = np.sin(angles) / math.sqrt(H)
    table = np.block([[cosine, -sine], [sine, cosine]]).astype(np.float32)
    both = np.stack([table, table.T])
    high = both.astype(jnp.bfloat16)
    low = (both - high.astype(np.float32)).astype(jnp.bfloat16)
    return high, low


def split(x):
    high = x.astype(BF16)
    return high, (x - high.astype(F32)).astype(BF16)


def mm(a, b):
    return jnp.dot(a, b, preferred_element_type=F32)


def rows_mm(x, w_high, w_low, product=mm):
    rows = x.shape[0]
    high, low = split(x)
    both = product(jnp.concatenate([high, low], axis=0), w_high)
    return both[:rows] + both[rows:] + product(high, w_low)


def sublane_sum(x):
    return jnp.sum(x, axis=0, keepdims=True)


def rows_to_lanes(rows):
    return sublane_sum(jnp.transpose(rows))


def wide(ref, at, part):
    return jnp.concatenate([ref[at, 2 * part], ref[at, 2 * part + 1]], axis=1)


def pack_kernel(k_ref, cond_ref, out_ref, v, cond, sems):
    copies = [
        pltpu.make_async_copy(k_ref.at[KRY - 1], v, sems.at[0]),
        pltpu.make_async_copy(cond_ref, cond, sems.at[1]),
    ]
    for copy in copies:
        copy.start()
    for copy in copies:
        copy.wait()
    for b in range(out_ref.shape[0]):
        for t in range(2):
            cols = slice(BS * b + LANES * t, BS * b + LANES * (t + 1))
            out_ref[b, t] = v[0, :, cols]
            out_ref[b, 2 + t] = v[1, :, cols]
            out_ref[b, 4 + t] = cond[:, cols]


def turn_kernel(diag_ref, cap_ref, high_ref, low_ref, t_ref, cap_out, high_out, low_out, held, sem):
    copy = pltpu.make_async_copy(diag_ref.at[lax.axis_index(HARM)], held, sem)
    copy.start()
    cap_out[...] = cap_ref[...]
    high_out[...] = high_ref[...]
    low_out[...] = low_ref[...]
    copy.wait()
    t_ref[...] = jnp.transpose(held[...])


def gram_kernel(k_ref, gram_ref, rows):
    rows[...] = jnp.zeros_like(rows)
    chunks = k_ref.shape[3] // LANES
    for m in range(KRY):
        real = [None] * KRY
        imag = [None] * KRY
        for c in range(chunks):
            cols = slice(LANES * c, LANES * (c + 1))
            mr, mi = k_ref[m, 0, :, cols], k_ref[m, 1, :, cols]
            for n in range(m, KRY):
                nr, ni = (mr, mi) if n == m else (k_ref[n, 0, :, cols], k_ref[n, 1, :, cols])
                r = mr * nr + mi * ni
                real[n] = r if c == 0 else real[n] + r
                if n > m:
                    i = mr * ni - mi * nr
                    imag[n] = i if c == 0 else imag[n] + i
        for n in range(m, KRY):
            at = GRAM + KRY * m + n
            rows[at : at + 1] = sublane_sum(real[n])
            if n > m:
                at = GRAM + KRY * n + m
                rows[at : at + 1] = sublane_sum(imag[n])
    gram_ref[...] = rows_to_lanes(rows[...])


def named_code(names, blk):
    group = lax.div(names, blk)
    local = (names - group * blk).astype(F32)
    hit = (group == lax.axis_index(NODE)) & (names >= 0)

    def over_all(x, reduce):
        return reduce(reduce(x, axis=1, keepdims=True), axis=0, keepdims=True)

    least = over_all(jnp.where(hit, local, blk - 1.0), jnp.min)
    greatest = over_all(jnp.where(hit, local, 0.0), jnp.max)
    return jnp.broadcast_to(least * CODE + greatest, (8, LANES))


def column_kernel(got_ref, t_ref, cap_ref, high_ref, low_ref, names_ref, out_ref, e_ref):
    own = lax.axis_index(HARM)
    sources = got_ref.shape[0]
    powers = e_ref.shape[0]
    cond = jnp.concatenate([wide(got_ref, s, 2) for s in range(sources)], axis=0)
    mean = sublane_sum(cond) * (1.0 / H)
    d = 1.0 / mean
    u = jnp.concatenate([wide(got_ref, s, p) for p in range(2) for s in range(sources)], axis=0) * d
    power = t_ref[...] * (-d)
    for p in range(powers):
        e_ref[p, 0], e_ref[p, 1] = split(power)
        high, low = e_ref[p, 0], e_ref[p, 1]
        u = u + rows_mm(u, high, low)
        if p < powers - 1:
            power = mm(high, high) + mm(low, high) + mm(high, low)
    high, low = e_ref[powers - 1, 0], e_ref[powers - 1, 1]
    u = u + rows_mm(rows_mm(u, high, low), high, low)
    direct = rows_mm(u, e_ref[0, 0], e_ref[0, 1]) * (-mean)

    def transform(way, x):
        high, low = split(x)
        table = high_ref[way]
        return mm(table, high) + mm(table, low) + mm(low_ref[way], high)

    driven = transform(0, u) * jnp.concatenate([cond, cond], axis=0)
    image = direct + transform(1, driven)
    cap = cap_ref[pl.ds(pl.multiple_of(own * BS, BS), BS)].reshape(1, BS)
    harmonic = lax.broadcasted_iota(jnp.int32, (H, BS), 0)
    omega = jnp.where(harmonic < H // 2, harmonic, harmonic - H)
    react = omega.astype(F32) * cap
    real = image[:H] - react * u[H:]
    imag = image[H:] + react * u[:H]
    step = H // sources
    code = named_code(names_ref[...], sources)
    for s in range(sources):
        rows = slice(step * s, step * (s + 1))
        later = slice(H + step * s, H + step * (s + 1))
        for at, part in enumerate((real[rows], imag[rows], u[rows], u[later])):
            out_ref[s, 2 * at] = part[:, :LANES]
            out_ref[s, 2 * at + 1] = part[:, LANES:]
        out_ref[s, 8] = code


def select_kernel(back_ref, send_ref):
    me = lax.axis_index(NODE)
    groups = send_ref.shape[0]
    for at, offset in enumerate(OFFSETS):
        group = me - offset

        @pl.when((group >= 0) & (group < groups))
        def _():
            code = back_ref[at, 8, 0:1, 0:1][0, 0].astype(jnp.int32)
            least = lax.div(code, CODE)
            for slot, b in enumerate((least, code - least * CODE)):
                send_ref[group, slot] = back_ref[b, 4:8]


def halve_kernel(c_ref, near_ref, far_ref, held, halves, in_sems, out_sems):
    blk = held.shape[0]
    kept = near_ref.shape[0]
    order = [*range(kept, blk), *range(kept)]
    reads = [pltpu.make_async_copy(c_ref.at[b], held.at[b], in_sems.at[b]) for b in range(blk)]
    writes = {b: pltpu.make_async_copy(halves.at[b - kept], far_ref.at[b], out_sems.at[b - kept]) for b in order[: blk - kept]}
    for b in order:
        reads[b].start()
    for b in order:
        reads[b].wait()
        for j in range(NEIGH):
            high, low = split(jnp.transpose(held[b, j]))
            if b < kept:
                near_ref[b, j, 0], near_ref[b, j, 1] = high, low
            else:
                halves[b - kept, j, 0], halves[b - kept, j, 1] = high, low
        if b >= kept:
            writes[b].start()
    for write in writes.values():
        write.wait()


def image_kernel(
    names_ref, got_ref, near_ref, far_ref, back_ref, k_ref, gram_ref, image_ref, send_ref, least, rows, held, sems
):
    blk = names_ref.shape[1]
    kept = near_ref.shape[0]
    half = image_ref.shape[1]
    copies = {b: pltpu.make_async_copy(far_ref.at[b], held.at[b - kept], sems.at[b - kept]) for b in range(kept, blk)}
    for copy in copies.values():
        copy.start()
    for q in range(got_ref.shape[0]):
        least[q] = blk
    for j in range(NEIGH):
        for b in range(blk):
            name = names_ref[j, b]
            group = lax.div(name, blk)
            local = name - group * blk

            @pl.when(name >= 0)
            def _():
                least[group] = jnp.minimum(least[group], local)

    for b in range(blk):
        if b >= kept:
            copies[b].wait()
        halves, at = (near_ref, b) if b < kept else (held, b - kept)
        total = jnp.concatenate([wide(back_ref, b, 0), wide(back_ref, b, 1)], axis=0)
        for j in range(NEIGH):
            name = jnp.maximum(names_ref[j, b], 0)
            group = lax.div(name, blk)
            slot = jnp.where(name - group * blk == least[group], 0, 1)
            x = got_ref[group, slot]
            x = jnp.concatenate([jnp.concatenate([x[2 * p], x[2 * p + 1]], axis=1) for p in range(2)], axis=0)
            x = jnp.where(names_ref[j, b] >= 0, x, 0.0)
            total = total + rows_mm(x, halves[at, j, 0], halves[at, j, 1])
        cols = slice(b * BS, (b + 1) * BS)
        image_ref[0, :, cols] = total[:half]
        image_ref[1, :, cols] = total[half:]

    chunks = k_ref.shape[3] // LANES
    real = [None] * KRY
    imag = [None] * KRY
    squares = None
    for c in range(chunks):
        cols = slice(LANES * c, LANES * (c + 1))
        ir, ii = image_ref[0, :, cols], image_ref[1, :, cols]
        both = ir * ir + ii * ii
        squares = both if c == 0 else squares + both
        for m in range(KRY):
            mr, mi = k_ref[m, 0, :, cols], k_ref[m, 1, :, cols]
            r = mr * ir + mi * ii
            i = mr * ii - mi * ir
            real[m] = r if c == 0 else real[m] + r
            imag[m] = i if c == 0 else imag[m] + i
    rows[...] = jnp.zeros_like(rows)
    for m in range(KRY):
        rows[m : m + 1] = sublane_sum(real[m])
        rows[KRY + m : KRY + m + 1] = sublane_sum(imag[m])
    rows[2 * KRY : 2 * KRY + 1] = sublane_sum(squares)
    row = rows_to_lanes(rows[...]) + gram_ref[...]
    send_ref[...] = jnp.broadcast_to(row, send_ref.shape)


def rest_kernel(count, got_ref, image_ref, k_ref, vector_ref, proj_ref, norm_ref):
    totals = sublane_sum(got_ref[...]) * (1.0 / count)
    lane = lax.broadcasted_iota(jnp.int32, totals.shape, 1)

    def at(q):
        return jnp.broadcast_to(totals[:, q : q + 1], totals.shape)

    pr = [at(m) for m in range(KRY)]
    pi = [at(KRY + m) for m in range(KRY)]
    row_r = row_i = col_r = col_i = jnp.zeros_like(totals)
    row_of = (lane - GRAM) // KRY
    col_of = (lane - GRAM) - row_of * KRY
    for m in range(KRY):
        row_r = jnp.where(row_of == m, pr[m], row_r)
        row_i = jnp.where(row_of == m, pi[m], row_i)
        col_r = jnp.where(col_of == m, pr[m], col_r)
        col_i = jnp.where(col_of == m, pi[m], col_i)
    upper = row_r * col_r + row_i * col_i
    lower = col_i * row_r - col_r * row_i
    weight = jnp.where(row_of == col_of, upper, 2.0 * jnp.where(row_of < col_of, upper, lower))
    weight = jnp.where(lane >= GRAM, weight, 0.0)
    weight = jnp.where(lane < 2 * KRY, -2.0 * totals, weight)
    weight = jnp.where(lane == 2 * KRY, 1.0, weight)
    squares = jnp.sum(totals * weight, axis=1, keepdims=True)
    norm = jnp.sqrt(squares + 1e-06)
    norm_ref[...] = norm
    for m in range(KRY):
        proj_ref[0:1, m : m + 1] = pr[m][:, 0:1]
        proj_ref[1:2, m : m + 1] = pi[m][:, 0:1]
    half = k_ref.shape[2]
    scale = jnp.broadcast_to(1.0 / norm, (half, LANES))
    pr = [jnp.broadcast_to(x, (half, LANES)) for x in pr]
    pi = [jnp.broadcast_to(x, (half, LANES)) for x in pi]
    for c in range(k_ref.shape[3] // LANES):
        cols = slice(LANES * c, LANES * (c + 1))
        real, imag = image_ref[0, :, cols], image_ref[1, :, cols]
        for m in range(KRY):
            mr, mi = k_ref[m, 0, :, cols], k_ref[m, 1, :, cols]
            real = real - (pr[m] * mr - pi[m] * mi)
            imag = imag - (pr[m] * mi + pi[m] * mr)
        vector_ref[0, :, cols] = real * scale
        vector_ref[1, :, cols] = imag * scale


def struct(*dims, dtype=F32):
    return pltpu.VMEM(dims, dtype)


def far(*dims, dtype=F32):
    return jax.ShapeDtypeStruct(dims, dtype)


def near(x):
    return pltpu.with_memory_space_constraint(x, pltpu.VMEM)


def call(kernel, out_shape, in_specs, flops, scratch=(), out_specs=None, limit=60 * 1024 * 1024):
    single = not isinstance(out_shape, tuple)
    return pl.pallas_call(
        kernel,
        out_shape=out_shape,
        in_specs=in_specs,
        out_specs=out_specs or (VMEM if single else (VMEM,) * len(out_shape)),
        scratch_shapes=list(scratch),
        cost_estimate=pl.CostEstimate(flops=flops, bytes_accessed=1 << 20, transcendentals=0),
        compiler_params=pltpu.CompilerParams(vmem_limit_bytes=limit),
    )


def exchange(x, axes):
    return lax.all_to_all(x, axes, split_axis=0, concat_axis=0, tiled=True)


def per_device(krylov_basis, cond_time, capacity, diag_blocks, coupling, neighbours, pattern):
    h_dev = krylov_basis.shape[2]
    nodes_dev = krylov_basis.shape[3]
    blk = diag_blocks.shape[0]
    harm = lax.axis_size(HARM)
    groups = lax.axis_size(NODE)
    world = groups * harm
    names = jnp.where(pattern > 0, neighbours, -1).T
    lanes = [pltpu.VMEM((LANES, LANES), F32)]

    packed = call(
        pack_kernel,
        far(blk, 6, h_dev, LANES),
        [ANY, ANY],
        1 << 20,
        [
            pltpu.VMEM((2, h_dev, nodes_dev), F32),
            pltpu.VMEM((h_dev, nodes_dev), F32),
            pltpu.SemaphoreType.DMA((2,)),
        ],
    )(krylov_basis, cond_time)
    got = near(exchange(packed, HARM))
    pairs = [
        (g * harm + s, (g + offset) * harm + s)
        for s, offset in enumerate(OFFSETS)
        for g in range(groups)
        if 0 <= g + offset < groups
    ]
    named_by = lax.ppermute(names, NODE_HARM, pairs)
    high, low = spectral_tables()
    turned = call(
        turn_kernel,
        (
            struct(BS, BS),
            struct(*capacity.shape),
            struct(*high.shape, dtype=BF16),
            struct(*low.shape, dtype=BF16),
        ),
        [ANY] + [VMEM] * 3,
        1 << 24,
        [pltpu.VMEM((BS, BS), F32), pltpu.SemaphoreType.DMA],
    )(diag_blocks, capacity, jnp.asarray(high), jnp.asarray(low))
    send_cols = call(
        column_kernel,
        far(harm, 9, h_dev, LANES),
        [VMEM] * 6,
        1 << 29,
        [pltpu.VMEM((3, 2, BS, BS), BF16)],
    )(got, *map(near, turned), near(named_by))
    back = near(exchange(send_cols, HARM))
    send_named = call(select_kernel, struct(groups, 2, 4, h_dev, LANES), [VMEM], 1 << 10, limit=8 << 20)(back)
    named = near(exchange(near(send_named), NODE))
    gram = call(gram_kernel, far(1, LANES), [VMEM], 1 << 24, lanes)(krylov_basis)
    krylov = near(krylov_basis)
    kept = blk // 2
    room = 4 * blk
    near_halves, far_halves = call(
        halve_kernel,
        (
            struct(kept, NEIGH, 2, BS, BS, dtype=BF16),
            far(room, NEIGH, 2, BS, BS, dtype=BF16),
        ),
        [ANY],
        1 << 24,
        [
            pltpu.VMEM(coupling.shape, F32),
            pltpu.VMEM((blk - kept, NEIGH, 2, BS, BS), BF16),
            pltpu.SemaphoreType.DMA((blk,)),
            pltpu.SemaphoreType.DMA((blk - kept,)),
        ],
        out_specs=(VMEM, ANY),
    )(coupling)
    image, send_sums = call(
        image_kernel,
        (struct(2, h_dev, nodes_dev), struct(world, LANES)),
        [SMEM, VMEM, VMEM, ANY] + [VMEM] * 3,
        1 << 28,
        [
            pltpu.SMEM((groups,), jnp.int32),
            *lanes,
            pltpu.VMEM((blk - kept, NEIGH, 2, BS, BS), BF16),
            pltpu.SemaphoreType.DMA((blk - kept,)),
        ],
        limit=48 << 20,
    )(names, named, near(near_halves), far_halves, back, krylov, gram)
    sums = near(exchange(send_sums, NODE_HARM))
    count = world * h_dev * nodes_dev
    vector, proj, norm = call(
        lambda *refs: rest_kernel(count, *refs),
        (far(2, h_dev, nodes_dev), far(2, KRY), far(1, 1)),
        [VMEM] * 3,
        1 << 24,
        limit=48 << 20,
    )(sums, near(image), krylov)
    return vector, proj, norm.reshape(())


def solution(mesh):
    finer = Mesh(mesh.devices.reshape(4, 4, 4, 2), ("node_0", "node_1", "harm_0", "harm_1"))
    placed = (
        P(None, None, HARM, NODE),
        P(HARM, NODE),
        P(NODE),
        P(NODE, None, None),
        P(NODE, None, None, None),
        P(NODE, None),
        P(NODE, None),
    )

    return jax.shard_map(
        per_device,
        mesh=finer,
        in_specs=placed,
        out_specs=(P(None, HARM, NODE), P(), P()),
        check_vma=False,
    )
```

time: 98.6 us -> 71.7 us (0.73)
  blocking collectives: 54.1 us -> 27 us
  Pallas kernels: 29.6 us -> 16.5 us
  starting transfers between devices: 7.41 us -> 19.2 us
  waiting for transfers between devices: 0.23 us -> 3.95 us
  local copies, waits for them, and re-layouts: 5.38 us -> 2.92 us
    all_to_all x4 -> x2, blocking collectives: 54.1 us -> 27 us  [exchange(): return lax.all_to_all(x, axes, split_axis=0, concat_axis=0, tiled=True)]
    pallas_call x5 -> x7, Pallas kernels: 24.3 us -> 13.4 us  [the longest x1 2.83 us: per_device(): call(halve_kernel, (struct(kept, NEIGH, 2, BS, BS, dtype=BF16), far(room,...]
    all_to_all x1 -> x2, starting transfers between devices: 7.41 us -> 14.6 us  [exchange(): return lax.all_to_all(x, axes, split_axis=0, concat_axis=0, tiled=True)]
    ppermute x0 -> x1, starting transfers between devices: none -> 4.64 us  [per_device(): named_by = lax.ppermute(names, NODE_HARM, pairs)]
    all_to_all x1 -> x2, waiting for transfers between devices: 0.23 us -> 3.95 us  [exchange(): return lax.all_to_all(x, axes, split_axis=0, concat_axis=0, tiled=True)]
    pallas_call x1, Pallas kernels: 5.27 us -> 3.15 us  [per_device(): call(image_kernel, (struct(2, h_dev, nodes_dev), struct(world, LANES)), [...]
    reshape x1 -> x0, local copies, waits for them, and re-layouts: 1.3 us -> none  [per_device(): capacity.reshape(blk, BS)]
  transfers between devices with their start and end apart: 1 -> 3, of which waited for: 1 -> 1; matrix products, arithmetic and copies ran while one was open for 2% -> 1% of each run, Pallas kernels for 4% -> 10%
where the time goes in v2:
time: 71.7 us; the launch traced here: 71 us
  blocking collectives  27 us (38%)
  starting transfers between devices  19.2 us (27%)
  Pallas kernels  16.5 us (23%)
  waiting for transfers between devices  3.95 us (6%)
  local copies, waits for them, and re-layouts  2.92 us (4%)
    all_to_all x2, blocking collectives, exchange(): return lax.all_to_all(x, axes, split_axis=0, concat_axis=0, tiled=True)  27 us
    all_to_all x2, starting transfers between devices, exchange(): return lax.all_to_all(x, axes, split_axis=0, concat_axis=0, tiled=True)  14.6 us
    ppermute x1, starting transfers between devices, per_device(): named_by = lax.ppermute(names, NODE_HARM, pairs)  4.64 us
    all_to_all x2, waiting for transfers between devices, exchange(): return lax.all_to_all(x, axes, split_axis=0, concat_axis=0, tiled=True)  3.95 us
    pallas_call x1, Pallas kernels, per_device(): call(image_kernel, (struct(2, h_dev, nodes_dev), struct(world, LANES)), [...  3.15 us
    unnamed x8, local copies, waits for them, and re-layouts  2.92 us
    pallas_call x1, Pallas kernels, per_device(): call(halve_kernel, (struct(kept, NEIGH, 2, BS, BS, dtype=BF16), far(room,...  2.83 us
    pallas_call x1, Pallas kernels, per_device(): call(column_kernel, far(harm, 9, h_dev, LANES), [VMEM] * 6, 1 << 29, [plt...  2.6 us
  transfers between devices with their start and end apart: 3, of which 1 were waited for; matrix products, arithmetic and copies ran while one was open for 1% of the time, Pallas kernels for 10%

profile of v2, /device:TPU:1, one launch (start us, length us, event | category | flops | bytes accessed | tf_op | source)
XLA Modules:
  0.0 71.0 jit_solution(12910758499300300976)
XLA Ops:
  0.6 1.6 %shard_map.112 = f32[8,6,8,128]{3,2,1,0:T(8,128)} custom-call(f32[8,2,8,2048]{3,2,1,0:T(8,128)} %refs_2_.1, f32[8,2048]{1,0:T(8,128)} %cond_ref.1), custom_call_target="tpu_custom_call" | custom-call | flops 1048576 | bytes 1048576 | tf_op jit(solution)/shard_map/pallas_call | solution.py:359
  2.3 6.8 %all-to-all-start = ((f32[8,6,8,128]{3,2,1,0:T(8,128)}), f32[8,6,8,128]{3,2,1,0:T(8,128)S(1)}, u32[]{:S(2)}, u32[]{:S(2)}) async-start(f32[8,6,8,128]{3,2,1,0:T(8,128)} %shard_map.112), calls=%async_computation | async-start | bytes 393216 | tf_op jit(solution)/shard_map/all_to_all | solution.py:346
  9.1 0.7 fusion.names_ref
  9.8 4.6 %collective-permute-start = (s32[2,8]{1,0:T(2,128)S(1)}, s32[2,8]{1,0:T(2,128)S(1)}, u32[]{:S(2)}, u32[]{:S(2)}) collective-permute-start(s32[2,8]{1,0:T(2,128)S(1)} %fusion.names_ref), channel_id=1, source_target_pairs={{0,8},{8,16},{16,24},{24,32},{32,40},{40,48},{48,56},{56,64},{64,7... | collective-permute-start | bytes 200 | tf_op jit(solution)/shard_map/ppermute | solution.py:377
  14.4 2.0 %shard_map.113 = (f32[256,256]{1,0:T(8,128)S(1)}, f32[2048]{0:T(1024)S(1)}, bf16[2,128,128]{2,1,0:T(8,128)(2,1)S(1)}, bf16[2,128,128]{2,1,0:T(8,128)(2,1)S(1)}) custom-call(f32[8,256,256]{2,1,0:T(8,128)} %diag_ref.1, f32[2048]{0:T(1024)} %cap_ref.1, bf16[2,128,128]{2,1,0:T(8,128)(2,1)} %constant.8.clone.high_ref, bf16[2,128,128]{2,1,0:T(8,128)(2,1)} %constant.9.clone.low_ref), custom_call_target="tpu_custom_call" | custom-call | flops 16777216 | bytes 1048576 | tf_op jit(solution)/shard_map/pallas_call | solution.py:379
  16.4 0.0 collective-permute-done.names_ref
  16.4 0.0 all-to-all-done.got_ref
  16.4 2.6 %shard_map.114 = f32[8,9,8,128]{3,2,1,0:T(8,128)} custom-call(f32[8,6,8,128]{3,2,1,0:T(8,128)S(1)} %all-to-all-done.got_ref, f32[256,256]{1,0:T(8,128)S(1)} %get-tuple-element.14.t_ref, f32[2048]{0:T(1024)S(1)} %get-tuple-element.15.cap_ref, bf16[2,128,128]{2,1,0:T(8,128)(2,1)S(1)} %get-tuple-element.16.high_ref, ...), custom_call_target="tpu_custom_call" | custom-call | flops 536870912 | bytes 1048576 | tf_op jit(solution)/shard_map/pallas_call | solution.py:391
  19.0 0.0 copy-start
  19.0 12.5 %all_to_all.26.back_ref = f32[8,9,8,128]{3,2,1,0:T(8,128)S(1)} all-to-all(f32[8,9,8,128]{3,2,1,0:T(8,128)} %shard_map.114), channel_id=1, replica_groups=mesh['node_0'=4,'node_1'=4,'harm_0'=4,'harm_1'=2] {'harm_0','harm_1'}, dimensions={0} | all-to-all | bytes 589824 | tf_op jit(solution)/shard_map/all_to_all | solution.py:346
  31.6 0.9 %shard_map.115 = f32[16,2,4,8,128]{4,3,2,1,0:T(8,128)} custom-call(f32[8,9,8,128]{3,2,1,0:T(8,128)S(1)} %all_to_all.26.back_ref), custom_call_target="tpu_custom_call" | custom-call | flops 1024 | bytes 1048576 | tf_op jit(solution)/shard_map/pallas_call | solution.py:399
  32.5 7.8 %all-to-all-start.2 = ((f32[16,2,4,8,128]{4,3,2,1,0:T(8,128)}), f32[16,2,4,8,128]{4,3,2,1,0:T(8,128)S(1)}, u32[]{:S(2)}, u32[]{:S(2)}) async-start(f32[16,2,4,8,128]{4,3,2,1,0:T(8,128)} %shard_map.115), calls=%async_computation.2 | async-start | bytes 1048576 | tf_op jit(solution)/shard_map/all_to_all | solution.py:346
  40.3 2.4 %shard_map.117.gram_ref = f32[1,128]{1,0:T(1,128)} custom-call(f32[8,2,8,2048]{3,2,1,0:T(8,128)} %refs_2_.1), custom_call_target="tpu_custom_call" | custom-call | flops 16777216 | bytes 1048576 | tf_op jit(solution)/shard_map/pallas_call | solution.py:401
  42.7 0.0 copy-start.3
  42.7 2.8 %shard_map.116 = (bf16[4,2,2,256,256]{4,3,2,1,0:T(8,128)(2,1)S(1)}, bf16[32,2,2,256,256]{4,3,2,1,0:T(8,128)(2,1)}) custom-call(f32[8,2,256,256]{3,2,1,0:T(8,128)} %c_ref.1), custom_call_target="tpu_custom_call" | custom-call | flops 16777216 | bytes 1048576 | tf_op jit(solution)/shard_map/pallas_call | solution.py:405
  45.6 0.0 copy-start.1
  45.6 1.3 %copy-done.1 = bf16[4,2,2,256,256]{4,3,2,1,0:T(8,128)(2,1)} copy-done((bf16[4,2,2,256,256]{4,3,2,1,0:T(8,128)(2,1)}, bf16[4,2,2,256,256]{4,3,2,1,0:T(8,128)(2,1)S(1)}, u32[]{:S(2)}) %copy-start.1) | copy-done | bytes 2097176
  46.9 3.9 %all-to-all-done.2.got_ref = f32[16,2,4,8,128]{4,3,2,1,0:T(8,128)S(1)} async-done(((f32[16,2,4,8,128]{4,3,2,1,0:T(8,128)}), f32[16,2,4,8,128]{4,3,2,1,0:T(8,128)S(1)}, u32[]{:S(2)}, u32[]{:S(2)}) %all-to-all-start.2) | async-done | bytes 524320 | tf_op jit(solution)/shard_map/all_to_all | solution.py:346
  50.8 0.0 copy-done
  50.8 0.0 copy-done.3
  50.8 0.0 copy-start.2
  50.8 1.6 %copy-done.2 = bf16[4,2,2,256,256]{4,3,2,1,0:T(8,128)(2,1)S(1)} copy-done((bf16[4,2,2,256,256]{4,3,2,1,0:T(8,128)(2,1)S(1)}, bf16[4,2,2,256,256]{4,3,2,1,0:T(8,128)(2,1)}, u32[]{:S(2)}) %copy-start.2) | copy-done | bytes 2097176
  52.4 3.1 %shard_map.118 = (f32[2,8,2048]{2,1,0:T(8,128)S(1)}, f32[128,128]{1,0:T(8,128)S(1)}) custom-call(s32[2,8]{1,0:T(2,128)S(1)} %fusion.names_ref, f32[16,2,4,8,128]{4,3,2,1,0:T(8,128)S(1)} %all-to-all-done.2.got_ref, bf16[4,2,2,256,256]{4,3,2,1,0:T(8,128)(2,1)S(1)} %copy-done.2, bf16[32,2,2,256,256]{4,3,2,1,0:T(8,128)(2,1)} %get-tuple-element.19.far_ref, ...), custom_call_target="tpu_custom_call" | custom-call | flops 268435456 | bytes 1048576 | tf_op jit(solution)/shard_map/pallas_call | solution.py:421
  55.6 14.4 %all_to_all.27 = f32[128,1,128]{2,1,0:T(1,128)S(1)} all-to-all(f32[128,1,128]{2,1,0:T(1,128)S(1)} %bitcast.8), channel_id=1, replica_groups=mesh['node_0'=4,'node_1'=4,'harm_0'=4,'harm_1'=2] {'node_0','node_1','ha..., dimensions={0} | all-to-all | bytes 131072 | tf_op jit(solution)/shard_map/all_to_all | solution.py:346
  70.0 1.0 %shard_map.119 = (f32[2,8,2048]{2,1,0:T(8,128)}, f32[2,8]{1,0:T(2,128)}, f32[1,1]{1,0:T(1,128)}) custom-call(f32[128,128]{1,0:T(8,128)S(1)} %bitcast.7, f32[2,8,2048]{2,1,0:T(8,128)S(1)} %get-tuple-element.21.refs_1_, f32[8,2,8,2048]{3,2,1,0:T(8,128)S(1)} %copy-done), custom_call_target="tpu_custom_call" | custom-call | flops 16777216 | bytes 1048576 | tf_op jit(solution)/shard_map/pallas_call | solution.py:436
Async XLA Ops:
  2.3 14.2 %all-to-all-start = ((f32[8,6,8,128]{3,2,1,0:T(8,128)}), f32[8,6,8,128]{3,2,1,0:T(8,128)S(1)}, u32[]{:S(2)}, u32[]{:S(2)}) async-start(f32[8,6,8,128]{3,2,1,0:T(8,128)} %shard_map.112), calls=%async_computation | async-start | bytes 393216 | tf_op jit(solution)/shard_map/all_to_all | solution.py:346
  9.8 6.6 %collective-permute-start = (s32[2,8]{1,0:T(2,128)S(1)}, s32[2,8]{1,0:T(2,128)S(1)}, u32[]{:S(2)}, u32[]{:S(2)}) collective-permute-start(s32[2,8]{1,0:T(2,128)S(1)} %fusion.names_ref), channel_id=1, source_target_pairs={{0,8},{8,16},{16,24},{24,32},{32,40},{40,48},{48,56},{56,64},{64,7... | collective-permute-start | bytes 200 | tf_op jit(solution)/shard_map/ppermute | solution.py:377
  19.0 31.8 %copy-start = (f32[8,2,8,2048]{3,2,1,0:T(8,128)S(1)}, f32[8,2,8,2048]{3,2,1,0:T(8,128)}, u32[]{:S(2)}) copy-start(f32[8,2,8,2048]{3,2,1,0:T(8,128)} %refs_2_.1) | copy-start | bytes 3145732
  32.5 18.3 %all-to-all-start.2 = ((f32[16,2,4,8,128]{4,3,2,1,0:T(8,128)}), f32[16,2,4,8,128]{4,3,2,1,0:T(8,128)S(1)}, u32[]{:S(2)}, u32[]{:S(2)}) async-start(f32[16,2,4,8,128]{4,3,2,1,0:T(8,128)} %shard_map.115), calls=%async_computation.2 | async-start | bytes 1048576 | tf_op jit(solution)/shard_map/all_to_all | solution.py:346
  42.7 8.1 %copy-start.3 = (f32[1,128]{1,0:T(1,128)S(1)}, f32[1,128]{1,0:T(1,128)}, u32[]{:S(2)}) copy-start(f32[1,128]{1,0:T(1,128)} %shard_map.117.gram_ref) | copy-start | bytes 1540
  45.6 1.3 %copy-start.1 = (bf16[4,2,2,256,256]{4,3,2,1,0:T(8,128)(2,1)}, bf16[4,2,2,256,256]{4,3,2,1,0:T(8,128)(2,1)S(1)}, u32[]{:S(2)}) copy-start(bf16[4,2,2,256,256]{4,3,2,1,0:T(8,128)(2,1)S(1)} %get-tuple-element.18.near_ref) | copy-start | bytes 6291460
  50.8 1.6 %copy-start.2 = (bf16[4,2,2,256,256]{4,3,2,1,0:T(8,128)(2,1)S(1)}, bf16[4,2,2,256,256]{4,3,2,1,0:T(8,128)(2,1)}, u32[]{:S(2)}) copy-start(bf16[4,2,2,256,256]{4,3,2,1,0:T(8,128)(2,1)} %copy-done.1) | copy-start | bytes 6291460

commit v3 on v2

--- a/solution.py
+++ b/solution.py
@@ -67,15 +67,18 @@
     return jnp.concatenate([ref[at, 2 * part], ref[at, 2 * part + 1]], axis=1)
 
 
-def pack_kernel(k_ref, cond_ref, out_ref, v, cond, sems):
+def pack_kernel(k_ref, cond_ref, nb_ref, pat_ref, out_ref, names_ref, v, cond, nb, pat, sems):
     copies = [
-        pltpu.make_async_copy(k_ref.at[KRY - 1], v, sems.at[0]),
-        pltpu.make_async_copy(cond_ref, cond, sems.at[1]),
+        pltpu.make_async_copy(source, target, sems.at[at])
+        for at, (source, target) in enumerate(
+            ((k_ref.at[KRY - 1], v), (cond_ref, cond), (nb_ref, nb), (pat_ref, pat))
+        )
     ]
     for copy in copies:
         copy.start()
     for copy in copies:
         copy.wait()
+    names_ref[...] = jnp.where(pat[...] > 0, nb[...], -1)
     for b in range(out_ref.shape[0]):
         for t in range(2):
             cols = slice(BS * b + LANES * t, BS * b + LANES * (t + 1))
@@ -132,12 +135,10 @@
     return jnp.broadcast_to(least * CODE + greatest, (8, LANES))
 
 
-def column_kernel(got_ref, t_ref, cap_ref, high_ref, low_ref, names_ref, out_ref, e_ref):
-    own = lax.axis_index(HARM)
+def solve_kernel(got_ref, t_ref, u_ref, direct_ref, e_ref):
     sources = got_ref.shape[0]
     powers = e_ref.shape[0]
-    cond = jnp.concatenate([wide(got_ref, s, 2) for s in range(sources)], axis=0)
-    mean = sublane_sum(cond) * (1.0 / H)
+    mean = sublane_sum(conductance(got_ref)) * (1.0 / H)
     d = 1.0 / mean
     u = jnp.concatenate([wide(got_ref, s, p) for p in range(2) for s in range(sources)], axis=0) * d
     power = t_ref[...] * (-d)
@@ -149,7 +150,19 @@
             power = mm(high, high) + mm(low, high) + mm(high, low)
     high, low = e_ref[powers - 1, 0], e_ref[powers - 1, 1]
     u = u + rows_mm(rows_mm(u, high, low), high, low)
-    direct = rows_mm(u, e_ref[0, 0], e_ref[0, 1]) * (-mean)
+    u_ref[...] = u
+    direct_ref[...] = rows_mm(u, e_ref[0, 0], e_ref[0, 1]) * (-mean)
+
+
+def conductance(got_ref):
+    return jnp.concatenate([wide(got_ref, s, 2) for s in range(got_ref.shape[0])], axis=0)
+
+
+def column_kernel(got_ref, u_ref, direct_ref, cap_ref, high_ref, low_ref, names_ref, out_ref):
+    own = lax.axis_index(HARM)
+    sources = got_ref.shape[0]
+    u = u_ref[...]
+    cond = conductance(got_ref)
 
     def transform(way, x):
         high, low = split(x)
@@ -157,7 +170,7 @@
         return mm(table, high) + mm(table, low) + mm(low_ref[way], high)
 
     driven = transform(0, u) * jnp.concatenate([cond, cond], axis=0)
-    image = direct + transform(1, driven)
+    image = direct_ref[...] + transform(1, driven)
     cap = cap_ref[pl.ds(pl.multiple_of(own * BS, BS), BS)].reshape(1, BS)
     harmonic = lax.broadcasted_iota(jnp.int32, (H, BS), 0)
     omega = jnp.where(harmonic < H // 2, harmonic, harmonic - H)
@@ -175,7 +188,13 @@
         out_ref[s, 8] = code
 
 
-def select_kernel(back_ref, send_ref):
+def pass_kernel(back_ref, halves_ref, mark_ref, passed_ref):
+    del halves_ref, passed_ref
+    mark_ref[...] = back_ref[0, 8]
+
+
+def select_kernel(back_ref, mark_ref, send_ref):
+    del mark_ref
     me = lax.axis_index(NODE)
     groups = send_ref.shape[0]
     for at, offset in enumerate(OFFSETS):
@@ -189,37 +208,24 @@
                 send_ref[group, slot] = back_ref[b, 4:8]
 
 
-def halve_kernel(c_ref, near_ref, far_ref, held, halves, in_sems, out_sems):
+def halve_kernel(c_ref, out_ref, held, halves, in_sems, out_sems):
     blk = held.shape[0]
-    kept = near_ref.shape[0]
-    order = [*range(kept, blk), *range(kept)]
     reads = [pltpu.make_async_copy(c_ref.at[b], held.at[b], in_sems.at[b]) for b in range(blk)]
-    writes = {b: pltpu.make_async_copy(halves.at[b - kept], far_ref.at[b], out_sems.at[b - kept]) for b in order[: blk - kept]}
-    for b in order:
-        reads[b].start()
-    for b in order:
+    writes = [pltpu.make_async_copy(halves.at[b], out_ref.at[b], out_sems.at[b]) for b in range(blk)]
+    for read in reads:
+        read.start()
+    for b in range(blk):
         reads[b].wait()
         for j in range(NEIGH):
-            high, low = split(jnp.transpose(held[b, j]))
-            if b < kept:
-                near_ref[b, j, 0], near_ref[b, j, 1] = high, low
-            else:
-                halves[b - kept, j, 0], halves[b - kept, j, 1] = high, low
-        if b >= kept:
-            writes[b].start()
-    for write in writes.values():
+            halves[b, j, 0], halves[b, j, 1] = split(jnp.transpose(held[b, j]))
+        writes[b].start()
+    for write in writes:
         write.wait()
 
 
-def image_kernel(
-    names_ref, got_ref, near_ref, far_ref, back_ref, k_ref, gram_ref, image_ref, send_ref, least, rows, held, sems
-):
-    blk = names_ref.shape[1]
-    kept = near_ref.shape[0]
+def image_kernel(names_ref, got_ref, halves_ref, back_ref, k_ref, gram_ref, image_ref, send_ref, least, rows):
+    blk = halves_ref.shape[0]
     half = image_ref.shape[1]
-    copies = {b: pltpu.make_async_copy(far_ref.at[b], held.at[b - kept], sems.at[b - kept]) for b in range(kept, blk)}
-    for copy in copies.values():
-        copy.start()
     for q in range(got_ref.shape[0]):
         least[q] = blk
     for j in range(NEIGH):
@@ -233,9 +239,6 @@
                 least[group] = jnp.minimum(least[group], local)
 
     for b in range(blk):
-        if b >= kept:
-            copies[b].wait()
-        halves, at = (near_ref, b) if b < kept else (held, b - kept)
         total = jnp.concatenate([wide(back_ref, b, 0), wide(back_ref, b, 1)], axis=0)
         for j in range(NEIGH):
             name = jnp.maximum(names_ref[j, b], 0)
@@ -244,7 +247,7 @@
             x = got_ref[group, slot]
             x = jnp.concatenate([jnp.concatenate([x[2 * p], x[2 * p + 1]], axis=1) for p in range(2)], axis=0)
             x = jnp.where(names_ref[j, b] >= 0, x, 0.0)
-            total = total + rows_mm(x, halves[at, j, 0], halves[at, j, 1])
+            total = total + rows_mm(x, halves_ref[b, j, 0], halves_ref[b, j, 1])
         cols = slice(b * BS, (b + 1) * BS)
         image_ref[0, :, cols] = total[:half]
         image_ref[1, :, cols] = total[half:]
@@ -329,7 +332,7 @@
     return pltpu.with_memory_space_constraint(x, pltpu.VMEM)
 
 
-def call(kernel, out_shape, in_specs, flops, scratch=(), out_specs=None, limit=60 * 1024 * 1024):
+def call(kernel, out_shape, in_specs, flops, scratch=(), out_specs=None, limit=60 * 1024 * 1024, aliases=None):
     single = not isinstance(out_shape, tuple)
     return pl.pallas_call(
         kernel,
@@ -339,6 +342,7 @@
         scratch_shapes=list(scratch),
         cost_estimate=pl.CostEstimate(flops=flops, bytes_accessed=1 << 20, transcendentals=0),
         compiler_params=pltpu.CompilerParams(vmem_limit_bytes=limit),
+        input_output_aliases=aliases or {},
     )
 
 
@@ -353,20 +357,22 @@
     harm = lax.axis_size(HARM)
     groups = lax.axis_size(NODE)
     world = groups * harm
-    names = jnp.where(pattern > 0, neighbours, -1).T
     lanes = [pltpu.VMEM((LANES, LANES), F32)]
-
-    packed = call(
+    krylov = near(krylov_basis)
+
+    packed, names = call(
         pack_kernel,
-        far(blk, 6, h_dev, LANES),
-        [ANY, ANY],
+        (far(blk, 6, h_dev, LANES), far(NEIGH, blk, dtype=jnp.int32)),
+        [ANY] * 4,
         1 << 20,
         [
             pltpu.VMEM((2, h_dev, nodes_dev), F32),
             pltpu.VMEM((h_dev, nodes_dev), F32),
-            pltpu.SemaphoreType.DMA((2,)),
+            pltpu.VMEM((NEIGH, blk), jnp.int32),
+            pltpu.VMEM((NEIGH, blk), jnp.int32),
+            pltpu.SemaphoreType.DMA((4,)),
         ],
-    )(krylov_basis, cond_time)
+    )(krylov_basis, cond_time, neighbours.T, pattern.T)
     got = near(exchange(packed, HARM))
     pairs = [
         (g * harm + s, (g + offset) * harm + s)
@@ -388,49 +394,52 @@
         1 << 24,
         [pltpu.VMEM((BS, BS), F32), pltpu.SemaphoreType.DMA],
     )(diag_blocks, capacity, jnp.asarray(high), jnp.asarray(low))
-    send_cols = call(
-        column_kernel,
-        far(harm, 9, h_dev, LANES),
-        [VMEM] * 6,
+    turned, *tables = turned
+    solved, direct = call(
+        solve_kernel,
+        (struct(2 * H, BS), struct(2 * H, BS)),
+        [VMEM] * 2,
         1 << 29,
         [pltpu.VMEM((3, 2, BS, BS), BF16)],
-    )(got, *map(near, turned), near(named_by))
+    )(got, near(turned))
+    send_cols = call(column_kernel, far(harm, 9, h_dev, LANES), [VMEM] * 7, 1 << 27)(
+        got, near(solved), near(direct), *map(near, tables), near(named_by)
+    )
     back = near(exchange(send_cols, HARM))
-    send_named = call(select_kernel, struct(groups, 2, 4, h_dev, LANES), [VMEM], 1 << 10, limit=8 << 20)(back)
-    named = near(exchange(near(send_named), NODE))
-    gram = call(gram_kernel, far(1, LANES), [VMEM], 1 << 24, lanes)(krylov_basis)
-    krylov = near(krylov_basis)
-    kept = blk // 2
-    room = 4 * blk
-    near_halves, far_halves = call(
+    halves = call(
         halve_kernel,
-        (
-            struct(kept, NEIGH, 2, BS, BS, dtype=BF16),
-            far(room, NEIGH, 2, BS, BS, dtype=BF16),
-        ),
+        far(blk, NEIGH, 2, BS, BS, dtype=BF16),
         [ANY],
         1 << 24,
         [
             pltpu.VMEM(coupling.shape, F32),
-            pltpu.VMEM((blk - kept, NEIGH, 2, BS, BS), BF16),
+            pltpu.VMEM((blk, NEIGH, 2, BS, BS), BF16),
             pltpu.SemaphoreType.DMA((blk,)),
-            pltpu.SemaphoreType.DMA((blk - kept,)),
+            pltpu.SemaphoreType.DMA((blk,)),
         ],
+        out_specs=ANY,
+    )(coupling)
+    mark, halves = call(
+        pass_kernel,
+        (struct(h_dev, LANES), far(*halves.shape, dtype=BF16)),
+        [VMEM, ANY],
+        1 << 10,
         out_specs=(VMEM, ANY),
-    )(coupling)
+        aliases={1: 1},
+    )(back, halves)
+    send_named = call(
+        select_kernel, struct(groups, 2, 4, h_dev, LANES), [VMEM, VMEM], 1 << 34, limit=32 << 20
+    )(back, near(mark))
+    named = near(exchange(near(send_named), NODE))
+    gram = call(gram_kernel, far(1, LANES), [VMEM], 1 << 24, lanes)(krylov)
     image, send_sums = call(
         image_kernel,
         (struct(2, h_dev, nodes_dev), struct(world, LANES)),
-        [SMEM, VMEM, VMEM, ANY] + [VMEM] * 3,
+        [SMEM] + [VMEM] * 5,
         1 << 28,
-        [
-            pltpu.SMEM((groups,), jnp.int32),
-            *lanes,
-            pltpu.VMEM((blk - kept, NEIGH, 2, BS, BS), BF16),
-            pltpu.SemaphoreType.DMA((blk - kept,)),
-        ],
-        limit=48 << 20,
-    )(names, named, near(near_halves), far_halves, back, krylov, gram)
+        [pltpu.SMEM((groups,), jnp.int32), *lanes],
+        limit=32 << 20,
+    )(names, named, near(halves), back, krylov, gram)
     sums = near(exchange(send_sums, NODE_HARM))
     count = world * h_dev * nodes_dev
     vector, proj, norm = call(

time: 71.7 us -> 68.7 us (0.958)
  blocking collectives: 27 us -> 14.7 us
  waiting for transfers between devices: 3.95 us -> 12.2 us
  starting transfers between devices: 19.2 us -> 22.9 us
  Pallas kernels: 16.5 us -> 14.7 us
    all_to_all x2 -> x1, blocking collectives: 27 us -> 14.7 us  [exchange(): return lax.all_to_all(x, axes, split_axis=0, concat_axis=0, tiled=True)]
    all_to_all x2 -> x3, waiting for transfers between devices: 3.95 us -> 12.2 us  [exchange(): return lax.all_to_all(x, axes, split_axis=0, concat_axis=0, tiled=True)]
    all_to_all x2 -> x3, starting transfers between devices: 14.6 us -> 18.3 us  [exchange(): return lax.all_to_all(x, axes, split_axis=0, concat_axis=0, tiled=True)]
    pallas_call x1, Pallas kernels: 3.15 us -> 1.51 us  [per_device(): call(image_kernel, (struct(2, h_dev, nodes_dev), struct(world, LANES)), [...]
    pallas_call x5 -> x7, Pallas kernels: 10.4 us -> 10.2 us  [the longest x1 3.65 us: per_device(): call(halve_kernel, far(blk, NEIGH, 2, BS, BS, dtype=BF16), [ANY], 1 << 24...]
  transfers between devices with their start and end apart: 3 -> 4, of which waited for: 1 -> 2; matrix products, arithmetic and copies ran while one was open for 1% -> 0% of each run, Pallas kernels for 10% -> 12%
where the time goes in v3:
time: 68.7 us; the launch traced here: 68.1 us
  starting transfers between devices  22.9 us (33%)
  Pallas kernels  14.7 us (21%)
  blocking collectives  14.7 us (21%)
  waiting for transfers between devices  12.2 us (18%)
  local copies, waits for them, and re-layouts  2.85 us (4%)
  between operations  0.72 us (1%)
    all_to_all x3, starting transfers between devices, exchange(): return lax.all_to_all(x, axes, split_axis=0, concat_axis=0, tiled=True)  18.3 us
    all_to_all x1, blocking collectives, exchange(): return lax.all_to_all(x, axes, split_axis=0, concat_axis=0, tiled=True)  14.7 us
    all_to_all x3, waiting for transfers between devices, exchange(): return lax.all_to_all(x, axes, split_axis=0, concat_axis=0, tiled=True)  12.2 us
    ppermute x1, starting transfers between devices, per_device(): named_by = lax.ppermute(names, NODE_HARM, pairs)  4.64 us
    pallas_call x1, Pallas kernels, per_device(): call(halve_kernel, far(blk, NEIGH, 2, BS, BS, dtype=BF16), [ANY], 1 << 24...  3.65 us
    unnamed x8, local copies, waits for them, and re-layouts  2.85 us
    pallas_call x1, Pallas kernels, per_device(): call(turn_kernel, (struct(BS, BS), struct(*capacity.shape), struct(*high....  1.99 us
    pallas_call x1, Pallas kernels, per_device(): call(pack_kernel, (far(blk, 6, h_dev, LANES), far(NEIGH, blk, dtype=jnp.i...  1.64 us
  transfers between devices with their start and end apart: 4, of which 2 were waited for; matrix products, arithmetic and copies ran while one was open for 0% of the time, Pallas kernels for 12%

profile of v3, /device:TPU:1, one launch (start us, length us, event | category | flops | bytes accessed | tf_op | source)
XLA Modules:
  0.0 68.1 jit_solution(17180712955600734460)
XLA Ops:
  0.6 1.6 %shard_map.112 = (f32[8,6,8,128]{3,2,1,0:T(8,128)}, s32[2,8]{1,0:T(2,128)}) custom-call(f32[8,2,8,2048]{3,2,1,0:T(8,128)} %refs_2_.1, f32[8,2048]{1,0:T(8,128)} %cond_ref.1, s32[2,8]{1,0:T(2,128)} %bitcast.9, s32[2,8]{1,0:T(2,128)} %bitcast.10), custom_call_target="tpu_custom_call" | custom-call | flops 1048576 | bytes 1048576 | tf_op jit(solution)/shard_map/pallas_call | solution.py:363
  2.3 6.8 %all-to-all-start = ((f32[8,6,8,128]{3,2,1,0:T(8,128)}), f32[8,6,8,128]{3,2,1,0:T(8,128)S(1)}, u32[]{:S(2)}, u32[]{:S(2)}) async-start(f32[8,6,8,128]{3,2,1,0:T(8,128)} %get-tuple-element.19), calls=%async_computation | async-start | bytes 393216 | tf_op jit(solution)/shard_map/all_to_all | solution.py:350
  9.1 4.6 %collective-permute-start = (s32[2,8]{1,0:T(2,128)}, s32[2,8]{1,0:T(2,128)S(1)}, u32[]{:S(2)}, u32[]{:S(2)}) collective-permute-start(s32[2,8]{1,0:T(2,128)} %get-tuple-element.18.names_ref), channel_id=1, source_target_pairs={{0,8},{8,16},{16,24},{24,32},{32,40},{40,48},{48,56},{56,64},{64,7... | collective-permute-start | bytes 200 | tf_op jit(solution)/shard_map/ppermute | solution.py:383
  13.7 2.0 %shard_map.113 = (f32[256,256]{1,0:T(8,128)S(1)}, f32[2048]{0:T(1024)S(1)}, bf16[2,128,128]{2,1,0:T(8,128)(2,1)S(1)}, bf16[2,128,128]{2,1,0:T(8,128)(2,1)S(1)}) custom-call(f32[8,256,256]{2,1,0:T(8,128)} %diag_ref.1, f32[2048]{0:T(1024)} %cap_ref.1, bf16[2,128,128]{2,1,0:T(8,128)(2,1)} %constant.4.clone.high_ref, bf16[2,128,128]{2,1,0:T(8,128)(2,1)} %constant.5.clone.low_ref), custom_call_target="tpu_custom_call" | custom-call | flops 16777216 | bytes 1048576 | tf_op jit(solution)/shard_map/pallas_call | solution.py:385
  15.7 0.0 all-to-all-done.got_ref
  15.7 1.6 %shard_map.114 = (f32[128,256]{1,0:T(8,128)S(1)}, f32[128,256]{1,0:T(8,128)S(1)}) custom-call(f32[8,6,8,128]{3,2,1,0:T(8,128)S(1)} %all-to-all-done.got_ref, f32[256,256]{1,0:T(8,128)S(1)} %get-tuple-element.20.t_ref), custom_call_target="tpu_custom_call" | custom-call | flops 536870912 | bytes 1048576 | tf_op jit(solution)/shard_map/pallas_call | solution.py:398
  17.4 0.0 collective-permute-done.names_ref
  17.4 1.2 %shard_map.115 = f32[8,9,8,128]{3,2,1,0:T(8,128)} custom-call(f32[8,6,8,128]{3,2,1,0:T(8,128)S(1)} %all-to-all-done.got_ref, f32[128,256]{1,0:T(8,128)S(1)} %get-tuple-element.21.u_ref, f32[128,256]{1,0:T(8,128)S(1)} %get-tuple-element.22.direct_ref, f32[2048]{0:T(1024)S(1)} %get-tuple-element.23.cap_ref, ...), custom_call_target="tpu_custom_call" | custom-call | flops 134217728 | bytes 1048576 | tf_op jit(solution)/shard_map/pallas_call | solution.py:405
  18.5 3.7 %all-to-all-start.1 = ((f32[8,9,8,128]{3,2,1,0:T(8,128)}), f32[8,9,8,128]{3,2,1,0:T(8,128)S(1)}, u32[]{:S(2)}, u32[]{:S(2)}) async-start(f32[8,9,8,128]{3,2,1,0:T(8,128)} %shard_map.115), calls=%async_computation.1 | async-start | bytes 589824 | tf_op jit(solution)/shard_map/all_to_all | solution.py:350
  22.2 3.7 %shard_map.116.halves_ref = bf16[8,2,2,256,256]{4,3,2,1,0:T(8,128)(2,1)} custom-call(f32[8,2,256,256]{3,2,1,0:T(8,128)} %c_ref.1), custom_call_target="tpu_custom_call" | custom-call | flops 16777216 | bytes 1048576 | tf_op jit(solution)/shard_map/pallas_call | solution.py:409
  25.9 3.1 %all-to-all-done.1.back_ref = f32[8,9,8,128]{3,2,1,0:T(8,128)S(1)} async-done(((f32[8,9,8,128]{3,2,1,0:T(8,128)}), f32[8,9,8,128]{3,2,1,0:T(8,128)S(1)}, u32[]{:S(2)}, u32[]{:S(2)}) %all-to-all-start.1) | async-done | bytes 294944 | tf_op jit(solution)/shard_map/all_to_all | solution.py:350
  29.0 0.0 copy-start.1
  29.0 0.0 copy-start.3
  29.0 0.9 %shard_map.118 = f32[16,2,4,8,128]{4,3,2,1,0:T(8,128)} custom-call(f32[8,9,8,128]{3,2,1,0:T(8,128)S(1)} %all-to-all-done.1.back_ref, f32[8,128]{1,0:T(8,128)S(1)} %get-tuple-element.26.mark_ref), custom_call_target="tpu_custom_call" | custom-call | flops 17179869184 | bytes 1048576 | tf_op jit(solution)/shard_map/pallas_call | solution.py:430
  30.0 7.8 %all-to-all-start.2 = ((f32[16,2,4,8,128]{4,3,2,1,0:T(8,128)}), f32[16,2,4,8,128]{4,3,2,1,0:T(8,128)S(1)}, u32[]{:S(2)}, u32[]{:S(2)}) async-start(f32[16,2,4,8,128]{4,3,2,1,0:T(8,128)} %shard_map.118), calls=%async_computation.2 | async-start | bytes 1048576 | tf_op jit(solution)/shard_map/all_to_all | solution.py:350
  37.8 0.0 copy-done.1
  37.8 1.2 %shard_map.119.gram_ref = f32[1,128]{1,0:T(1,128)} custom-call(f32[8,2,8,2048]{3,2,1,0:T(8,128)S(1)} %copy-done.1), custom_call_target="tpu_custom_call" | custom-call | flops 16777216 | bytes 1048576 | tf_op jit(solution)/shard_map/pallas_call | solution.py:434
  39.0 9.1 %all-to-all-done.2.got_ref = f32[16,2,4,8,128]{4,3,2,1,0:T(8,128)S(1)} async-done(((f32[16,2,4,8,128]{4,3,2,1,0:T(8,128)}), f32[16,2,4,8,128]{4,3,2,1,0:T(8,128)S(1)}, u32[]{:S(2)}, u32[]{:S(2)}) %all-to-all-start.2) | async-done | bytes 524320 | tf_op jit(solution)/shard_map/all_to_all | solution.py:350
  48.1 0.0 copy-done.3
  48.1 0.0 copy-start
  48.1 2.2 %copy-done = bf16[8,2,2,256,256]{4,3,2,1,0:T(8,128)(2,1)S(1)} copy-done((bf16[8,2,2,256,256]{4,3,2,1,0:T(8,128)(2,1)S(1)}, bf16[8,2,2,256,256]{4,3,2,1,0:T(8,128)(2,1)}, u32[]{:S(2)}) %copy-start) | copy-done | bytes 4194328
  50.3 0.0 copy-start.2
  50.3 0.7 copy-done.2
  50.9 1.5 %shard_map.120 = (f32[2,8,2048]{2,1,0:T(8,128)S(1)}, f32[128,128]{1,0:T(8,128)S(1)}) custom-call(s32[2,8]{1,0:T(2,128)S(1)} %copy-done.3, f32[16,2,4,8,128]{4,3,2,1,0:T(8,128)S(1)} %all-to-all-done.2.got_ref, bf16[8,2,2,256,256]{4,3,2,1,0:T(8,128)(2,1)S(1)} %copy-done, f32[8,9,8,128]{3,2,1,0:T(8,128)S(1)} %all-to-all-done.1.back_ref, ...), custom_call_target="tpu_custom_call" | custom-call | flops 268435456 | bytes 1048576 | tf_op jit(solution)/shard_map/pallas_call | solution.py:435
  52.4 14.7 %all_to_all.26 = f32[128,1,128]{2,1,0:T(1,128)S(1)} all-to-all(f32[128,1,128]{2,1,0:T(1,128)S(1)} %bitcast.8), channel_id=1, replica_groups=mesh['node_0'=4,'node_1'=4,'harm_0'=4,'harm_1'=2] {'node_0','node_1','ha..., dimensions={0} | all-to-all | bytes 131072 | tf_op jit(solution)/shard_map/all_to_all | solution.py:350
  67.1 1.0 %shard_map.121 = (f32[2,8,2048]{2,1,0:T(8,128)}, f32[2,8]{1,0:T(2,128)}, f32[1,1]{1,0:T(1,128)}) custom-call(f32[128,128]{1,0:T(8,128)S(1)} %bitcast.7, f32[2,8,2048]{2,1,0:T(8,128)S(1)} %get-tuple-element.29.refs_1_, f32[8,2,8,2048]{3,2,1,0:T(8,128)S(1)} %copy-done.1), custom_call_target="tpu_custom_call" | custom-call | flops 16777216 | bytes 1048576 | tf_op jit(solution)/shard_map/pallas_call | solution.py:445
  (1 shorter events, 0.0 us)
Async XLA Ops:
  2.3 13.5 %all-to-all-start = ((f32[8,6,8,128]{3,2,1,0:T(8,128)}), f32[8,6,8,128]{3,2,1,0:T(8,128)S(1)}, u32[]{:S(2)}, u32[]{:S(2)}) async-start(f32[8,6,8,128]{3,2,1,0:T(8,128)} %get-tuple-element.19), calls=%async_computation | async-start | bytes 393216 | tf_op jit(solution)/shard_map/all_to_all | solution.py:350
  9.1 8.3 %collective-permute-start = (s32[2,8]{1,0:T(2,128)}, s32[2,8]{1,0:T(2,128)S(1)}, u32[]{:S(2)}, u32[]{:S(2)}) collective-permute-start(s32[2,8]{1,0:T(2,128)} %get-tuple-element.18.names_ref), channel_id=1, source_target_pairs={{0,8},{8,16},{16,24},{24,32},{32,40},{40,48},{48,56},{56,64},{64,7... | collective-permute-start | bytes 200 | tf_op jit(solution)/shard_map/ppermute | solution.py:383
  18.5 10.5 %all-to-all-start.1 = ((f32[8,9,8,128]{3,2,1,0:T(8,128)}), f32[8,9,8,128]{3,2,1,0:T(8,128)S(1)}, u32[]{:S(2)}, u32[]{:S(2)}) async-start(f32[8,9,8,128]{3,2,1,0:T(8,128)} %shard_map.115), calls=%async_computation.1 | async-start | bytes 589824 | tf_op jit(solution)/shard_map/all_to_all | solution.py:350
  29.0 8.7 %copy-start.1 = (f32[8,2,8,2048]{3,2,1,0:T(8,128)S(1)}, f32[8,2,8,2048]{3,2,1,0:T(8,128)}, u32[]{:S(2)}) copy-start(f32[8,2,8,2048]{3,2,1,0:T(8,128)} %refs_2_.1) | copy-start | bytes 3145732
  29.0 19.1 %copy-start.3 = (s32[2,8]{1,0:T(2,128)S(1)}, s32[2,8]{1,0:T(2,128)}, u32[]{:S(2)}) copy-start(s32[2,8]{1,0:T(2,128)} %get-tuple-element.18.names_ref) | copy-start | bytes 196
  30.0 18.1 %all-to-all-start.2 = ((f32[16,2,4,8,128]{4,3,2,1,0:T(8,128)}), f32[16,2,4,8,128]{4,3,2,1,0:T(8,128)S(1)}, u32[]{:S(2)}, u32[]{:S(2)}) async-start(f32[16,2,4,8,128]{4,3,2,1,0:T(8,128)} %shard_map.118), calls=%async_computation.2 | async-start | bytes 1048576 | tf_op jit(solution)/shard_map/all_to_all | solution.py:350
  48.1 2.2 %copy-start = (bf16[8,2,2,256,256]{4,3,2,1,0:T(8,128)(2,1)S(1)}, bf16[8,2,2,256,256]{4,3,2,1,0:T(8,128)(2,1)}, u32[]{:S(2)}) copy-start(bf16[8,2,2,256,256]{4,3,2,1,0:T(8,128)(2,1)} %get-tuple-element.27.halves_ref) | copy-start | bytes 12582916
  50.3 0.7 copy-start.2

commit v4 on v3

--- a/solution.py
+++ b/solution.py
@@ -87,14 +87,47 @@
             out_ref[b, 4 + t] = cond[:, cols]
 
 
-def turn_kernel(diag_ref, cap_ref, high_ref, low_ref, t_ref, cap_out, high_out, low_out, held, sem):
-    copy = pltpu.make_async_copy(diag_ref.at[lax.axis_index(HARM)], held, sem)
-    copy.start()
-    cap_out[...] = cap_ref[...]
-    high_out[...] = high_ref[...]
-    low_out[...] = low_ref[...]
-    copy.wait()
+def turn_kernel(
+    names_ref, diag_ref, cap_ref, high_ref, low_ref, t_ref, where_ref, cap_out, high_out, low_out, held, names, least, sems
+):
+    copies = [
+        pltpu.make_async_copy(source, target, sems.at[at])
+        for at, (source, target) in enumerate(
+            (
+                (diag_ref.at[lax.axis_index(HARM)], held),
+                (names_ref, names),
+                (cap_ref, cap_out),
+                (high_ref, high_out),
+                (low_ref, low_out),
+            )
+        )
+    ]
+    for copy in copies:
+        copy.start()
+    copies[1].wait()
+    blk = names.shape[1]
+    for q in range(least.shape[0]):
+        least[q] = blk
+    for j in range(NEIGH):
+        for b in range(blk):
+            name = names[j, b]
+            group = lax.div(name, blk)
+            local = name - group * blk
+
+            @pl.when(name >= 0)
+            def _():
+                least[group] = jnp.minimum(least[group], local)
+
+    for j in range(NEIGH):
+        for b in range(blk):
+            name = names[j, b]
+            group = lax.div(jnp.maximum(name, 0), blk)
+            slot = jnp.where(name - group * blk == least[group], 0, 1)
+            where_ref[j, b] = jnp.where(name >= 0, 2 * group + slot, -1)
+    copies[0].wait()
     t_ref[...] = jnp.transpose(held[...])
+    for copy in copies[2:]:
+        copy.wait()
 
 
 def gram_kernel(k_ref, gram_ref, rows):
@@ -188,13 +221,7 @@
         out_ref[s, 8] = code
 
 
-def pass_kernel(back_ref, halves_ref, mark_ref, passed_ref):
-    del halves_ref, passed_ref
-    mark_ref[...] = back_ref[0, 8]
-
-
-def select_kernel(back_ref, mark_ref, send_ref):
-    del mark_ref
+def select_kernel(back_ref, send_ref):
     me = lax.axis_index(NODE)
     groups = send_ref.shape[0]
     for at, offset in enumerate(OFFSETS):
@@ -223,30 +250,17 @@
         write.wait()
 
 
-def image_kernel(names_ref, got_ref, halves_ref, back_ref, k_ref, gram_ref, image_ref, send_ref, least, rows):
+def image_kernel(where_ref, got_ref, halves_ref, back_ref, k_ref, gram_ref, image_ref, send_ref, rows):
     blk = halves_ref.shape[0]
     half = image_ref.shape[1]
-    for q in range(got_ref.shape[0]):
-        least[q] = blk
-    for j in range(NEIGH):
-        for b in range(blk):
-            name = names_ref[j, b]
-            group = lax.div(name, blk)
-            local = name - group * blk
-
-            @pl.when(name >= 0)
-            def _():
-                least[group] = jnp.minimum(least[group], local)
-
     for b in range(blk):
         total = jnp.concatenate([wide(back_ref, b, 0), wide(back_ref, b, 1)], axis=0)
         for j in range(NEIGH):
-            name = jnp.maximum(names_ref[j, b], 0)
-            group = lax.div(name, blk)
-            slot = jnp.where(name - group * blk == least[group], 0, 1)
-            x = got_ref[group, slot]
+            at = where_ref[j : j + 1, b : b + 1][0, 0]
+            group = lax.div(jnp.maximum(at, 0), 2)
+            x = got_ref[group, jnp.maximum(at - 2 * group, 0)]
             x = jnp.concatenate([jnp.concatenate([x[2 * p], x[2 * p + 1]], axis=1) for p in range(2)], axis=0)
-            x = jnp.where(names_ref[j, b] >= 0, x, 0.0)
+            x = jnp.where(at >= 0, x, 0.0)
             total = total + rows_mm(x, halves_ref[b, j, 0], halves_ref[b, j, 1])
         cols = slice(b * BS, (b + 1) * BS)
         image_ref[0, :, cols] = total[:half]
@@ -362,7 +376,7 @@
 
     packed, names = call(
         pack_kernel,
-        (far(blk, 6, h_dev, LANES), far(NEIGH, blk, dtype=jnp.int32)),
+        (far(blk, 6, h_dev, LANES), struct(NEIGH, blk, dtype=jnp.int32)),
         [ANY] * 4,
         1 << 20,
         [
@@ -380,21 +394,28 @@
         for g in range(groups)
         if 0 <= g + offset < groups
     ]
-    named_by = lax.ppermute(names, NODE_HARM, pairs)
+    named_by = lax.ppermute(near(names), NODE_HARM, pairs)
     high, low = spectral_tables()
     turned = call(
         turn_kernel,
         (
             struct(BS, BS),
+            far(NEIGH, blk, dtype=jnp.int32),
             struct(*capacity.shape),
             struct(*high.shape, dtype=BF16),
             struct(*low.shape, dtype=BF16),
         ),
-        [ANY] + [VMEM] * 3,
+        [ANY] * 5,
         1 << 24,
-        [pltpu.VMEM((BS, BS), F32), pltpu.SemaphoreType.DMA],
-    )(diag_blocks, capacity, jnp.asarray(high), jnp.asarray(low))
-    turned, *tables = turned
+        [
+            pltpu.VMEM((BS, BS), F32),
+            pltpu.SMEM((NEIGH, blk), jnp.int32),
+            pltpu.SMEM((groups,), jnp.int32),
+            pltpu.SemaphoreType.DMA((5,)),
+        ],
+        out_specs=(VMEM, SMEM, VMEM, VMEM, VMEM),
+    )(names, diag_blocks, capacity, jnp.asarray(high), jnp.asarray(low))
+    turned, where, *tables = turned
     solved, direct = call(
         solve_kernel,
         (struct(2 * H, BS), struct(2 * H, BS)),
@@ -419,27 +440,19 @@
         ],
         out_specs=ANY,
     )(coupling)
-    mark, halves = call(
-        pass_kernel,
-        (struct(h_dev, LANES), far(*halves.shape, dtype=BF16)),
-        [VMEM, ANY],
-        1 << 10,
-        out_specs=(VMEM, ANY),
-        aliases={1: 1},
-    )(back, halves)
     send_named = call(
-        select_kernel, struct(groups, 2, 4, h_dev, LANES), [VMEM, VMEM], 1 << 34, limit=32 << 20
-    )(back, near(mark))
-    named = near(exchange(near(send_named), NODE))
+        select_kernel, struct(groups, 2, 4, h_dev, LANES), [VMEM], 1 << 34, limit=32 << 20
+    )(back)
+    named = exchange(near(send_named), NODE)
     gram = call(gram_kernel, far(1, LANES), [VMEM], 1 << 24, lanes)(krylov)
     image, send_sums = call(
         image_kernel,
         (struct(2, h_dev, nodes_dev), struct(world, LANES)),
-        [SMEM] + [VMEM] * 5,
+        [VMEM] * 6,
         1 << 28,
-        [pltpu.SMEM((groups,), jnp.int32), *lanes],
+        lanes,
         limit=32 << 20,
-    )(names, named, near(halves), back, krylov, gram)
+    )(near(where), near(named), near(halves), back, krylov, near(gram))
     sums = near(exchange(send_sums, NODE_HARM))
     count = world * h_dev * nodes_dev
     vector, proj, norm = call(

time: 68.7 us -> 67.7 us (0.985)
  blocking collectives: 14.7 us -> 25.4 us
  waiting for transfers between devices: 12.2 us -> 5.66 us
  starting transfers between devices: 22.9 us -> 19.2 us
  Pallas kernels: 14.7 us -> 13.9 us
    all_to_all x1 -> x2, blocking collectives: 14.7 us -> 25.4 us  [exchange(): return lax.all_to_all(x, axes, split_axis=0, concat_axis=0, tiled=True)]
    all_to_all x3 -> x2, waiting for transfers between devices: 12.2 us -> 5.66 us  [exchange(): return lax.all_to_all(x, axes, split_axis=0, concat_axis=0, tiled=True)]
    all_to_all x3 -> x2, starting transfers between devices: 18.3 us -> 14.6 us  [exchange(): return lax.all_to_all(x, axes, split_axis=0, concat_axis=0, tiled=True)]
    unnamed x8 -> x10, local copies, waits for them, and re-layouts: 2.85 us -> 2.21 us
    pallas_call x4 -> x3, Pallas kernels: 4.57 us -> 4.35 us  [the longest x1 1.76 us: per_device(): call(turn_kernel, (struct(BS, BS), far(NEIGH, blk, dtype=jnp.int32), stru...]
  transfers between devices with their start and end apart: 4 -> 3, of which waited for: 2 -> 1; matrix products, arithmetic and copies ran while one was open for 0% -> 0% of each run, Pallas kernels for 12% -> 12%
where the time goes in v4:
time: 67.7 us; the launch traced here: 67.2 us
  blocking collectives  25.4 us (38%)
  starting transfers between devices  19.2 us (28%)
  Pallas kernels  13.9 us (21%)
  waiting for transfers between devices  5.66 us (8%)
  local copies, waits for them, and re-layouts  2.21 us (3%)
  between operations  0.73 us (1%)
    all_to_all x2, blocking collectives, exchange(): return lax.all_to_all(x, axes, split_axis=0, concat_axis=0, tiled=True)  25.4 us
    all_to_all x2, starting transfers between devices, exchange(): return lax.all_to_all(x, axes, split_axis=0, concat_axis=0, tiled=True)  14.6 us
    all_to_all x2, waiting for transfers between devices, exchange(): return lax.all_to_all(x, axes, split_axis=0, concat_axis=0, tiled=True)  5.66 us
    ppermute x1, starting transfers between devices, per_device(): named_by = lax.ppermute(near(names), NODE_HARM, pairs)  4.64 us
    pallas_call x1, Pallas kernels, per_device(): call(halve_kernel, far(blk, NEIGH, 2, BS, BS, dtype=BF16), [ANY], 1 << 24...  3.66 us
    unnamed x10, local copies, waits for them, and re-layouts  2.21 us
    pallas_call x1, Pallas kernels, per_device(): call(turn_kernel, (struct(BS, BS), far(NEIGH, blk, dtype=jnp.int32), stru...  1.76 us
    pallas_call x1, Pallas kernels, per_device(): call(pack_kernel, (far(blk, 6, h_dev, LANES), struct(NEIGH, blk, dtype=jn...  1.65 us
  transfers between devices with their start and end apart: 3, of which 1 were waited for; matrix products, arithmetic and copies ran while one was open for 0% of the time, Pallas kernels for 12%

profile of v4, /device:TPU:1, one launch (start us, length us, event | category | flops | bytes accessed | tf_op | source)
XLA Modules:
  0.0 67.2 jit_solution(4253115364228034301)
XLA Ops:
  0.6 1.6 %shard_map.112 = (f32[8,6,8,128]{3,2,1,0:T(8,128)}, s32[2,8]{1,0:T(2,128)S(1)}) custom-call(f32[8,2,8,2048]{3,2,1,0:T(8,128)} %refs_2_.1, f32[8,2048]{1,0:T(8,128)} %cond_ref.1, s32[2,8]{1,0:T(2,128)} %bitcast.9, s32[2,8]{1,0:T(2,128)} %bitcast.10), custom_call_target="tpu_custom_call" | custom-call | flops 1048576 | bytes 1048576 | tf_op jit(solution)/shard_map/pallas_call | solution.py:377
  2.3 0.0 copy-start.3
  2.3 6.8 %all-to-all-start = ((f32[8,6,8,128]{3,2,1,0:T(8,128)}), f32[8,6,8,128]{3,2,1,0:T(8,128)S(1)}, u32[]{:S(2)}, u32[]{:S(2)}) async-start(f32[8,6,8,128]{3,2,1,0:T(8,128)} %get-tuple-element.19), calls=%async_computation | async-start | bytes 393216 | tf_op jit(solution)/shard_map/all_to_all | solution.py:364
  9.1 4.6 %collective-permute-start = (s32[2,8]{1,0:T(2,128)S(1)}, s32[2,8]{1,0:T(2,128)S(1)}, u32[]{:S(2)}, u32[]{:S(2)}) collective-permute-start(s32[2,8]{1,0:T(2,128)S(1)} %get-tuple-element.17.names_ref), channel_id=1, source_target_pairs={{0,8},{8,16},{16,24},{24,32},{32,40},{40,48},{48,56},{56,64},{64,7... | collective-permute-start | bytes 200 | tf_op jit(solution)/shard_map/ppermute | solution.py:397
  13.8 0.0 copy-done.3
  13.8 1.8 %shard_map.113 = (f32[256,256]{1,0:T(8,128)S(1)}, s32[2,8]{1,0:T(2,128)}, f32[2048]{0:T(1024)S(1)}, bf16[2,128,128]{2,1,0:T(8,128)(2,1)S(1)}, bf16[2,128,128]{2,1,0:T(8,128)(2,1)S(1)}) custom-call(s32[2,8]{1,0:T(2,128)} %copy-done.3, f32[8,256,256]{2,1,0:T(8,128)} %diag_ref.1, f32[2048]{0:T(1024)} %cap_ref.1, bf16[2,128,128]{2,1,0:T(8,128)(2,1)} %constant.4.clone.high_ref, ...), custom_call_target="tpu_custom_call" | custom-call | flops 16777216 | bytes 1048576 | tf_op jit(solution)/shard_map/pallas_call | solution.py:399
  15.5 0.0 all-to-all-done.got_ref
  15.5 1.6 %shard_map.114 = (f32[128,256]{1,0:T(8,128)S(1)}, f32[128,256]{1,0:T(8,128)S(1)}) custom-call(f32[8,6,8,128]{3,2,1,0:T(8,128)S(1)} %all-to-all-done.got_ref, f32[256,256]{1,0:T(8,128)S(1)} %get-tuple-element.20.t_ref), custom_call_target="tpu_custom_call" | custom-call | flops 536870912 | bytes 1048576 | tf_op jit(solution)/shard_map/pallas_call | solution.py:419
  17.2 0.0 collective-permute-done.names_ref
  17.2 1.2 %shard_map.115 = f32[8,9,8,128]{3,2,1,0:T(8,128)} custom-call(f32[8,6,8,128]{3,2,1,0:T(8,128)S(1)} %all-to-all-done.got_ref, f32[128,256]{1,0:T(8,128)S(1)} %get-tuple-element.21.u_ref, f32[128,256]{1,0:T(8,128)S(1)} %get-tuple-element.22.direct_ref, f32[2048]{0:T(1024)S(1)} %get-tuple-element.23.cap_ref, ...), custom_call_target="tpu_custom_call" | custom-call | flops 134217728 | bytes 1048576 | tf_op jit(solution)/shard_map/pallas_call | solution.py:426
  18.3 11.0 %all_to_all.26.back_ref = f32[8,9,8,128]{3,2,1,0:T(8,128)S(1)} all-to-all(f32[8,9,8,128]{3,2,1,0:T(8,128)} %shard_map.115), channel_id=1, replica_groups=mesh['node_0'=4,'node_1'=4,'harm_0'=4,'harm_1'=2] {'harm_0','harm_1'}, dimensions={0} | all-to-all | bytes 589824 | tf_op jit(solution)/shard_map/all_to_all | solution.py:364
  29.3 0.0 copy-start.1
  29.3 0.9 %shard_map.116 = f32[16,2,4,8,128]{4,3,2,1,0:T(8,128)} custom-call(f32[8,9,8,128]{3,2,1,0:T(8,128)S(1)} %all_to_all.26.back_ref), custom_call_target="tpu_custom_call" | custom-call | flops 17179869184 | bytes 1048576 | tf_op jit(solution)/shard_map/pallas_call | solution.py:443
  30.3 7.8 %all-to-all-start.2 = ((f32[16,2,4,8,128]{4,3,2,1,0:T(8,128)}), f32[16,2,4,8,128]{4,3,2,1,0:T(8,128)S(1)}, u32[]{:S(2)}, u32[]{:S(2)}) async-start(f32[16,2,4,8,128]{4,3,2,1,0:T(8,128)} %shard_map.116), calls=%async_computation.2 | async-start | bytes 1048576 | tf_op jit(solution)/shard_map/all_to_all | solution.py:364
  38.1 0.0 copy-done.1
  38.1 1.2 %shard_map.118.gram_ref = f32[1,128]{1,0:T(1,128)} custom-call(f32[8,2,8,2048]{3,2,1,0:T(8,128)S(1)} %copy-done.1), custom_call_target="tpu_custom_call" | custom-call | flops 16777216 | bytes 1048576 | tf_op jit(solution)/shard_map/pallas_call | solution.py:447
  39.3 0.0 copy-start.2
  39.3 0.0 copy-start.4
  39.3 3.7 %shard_map.117.halves_ref = bf16[8,2,2,256,256]{4,3,2,1,0:T(8,128)(2,1)} custom-call(f32[8,2,256,256]{3,2,1,0:T(8,128)} %c_ref.1), custom_call_target="tpu_custom_call" | custom-call | flops 16777216 | bytes 1048576 | tf_op jit(solution)/shard_map/pallas_call | solution.py:430
  42.9 5.7 %all-to-all-done.2.got_ref = f32[16,2,4,8,128]{4,3,2,1,0:T(8,128)S(1)} async-done(((f32[16,2,4,8,128]{4,3,2,1,0:T(8,128)}), f32[16,2,4,8,128]{4,3,2,1,0:T(8,128)S(1)}, u32[]{:S(2)}, u32[]{:S(2)}) %all-to-all-start.2) | async-done | bytes 524320 | tf_op jit(solution)/shard_map/all_to_all | solution.py:364
  48.6 0.0 copy-done.2
  48.6 0.0 copy-done.4
  48.6 0.0 copy-start
  48.6 2.2 %copy-done = bf16[8,2,2,256,256]{4,3,2,1,0:T(8,128)(2,1)S(1)} copy-done((bf16[8,2,2,256,256]{4,3,2,1,0:T(8,128)(2,1)S(1)}, bf16[8,2,2,256,256]{4,3,2,1,0:T(8,128)(2,1)}, u32[]{:S(2)}) %copy-start) | copy-done | bytes 4194328
  50.8 1.0 %shard_map.119 = (f32[2,8,2048]{2,1,0:T(8,128)S(1)}, f32[128,128]{1,0:T(8,128)S(1)}) custom-call(s32[2,8]{1,0:T(2,128)S(1)} %copy-done.4, f32[16,2,4,8,128]{4,3,2,1,0:T(8,128)S(1)} %all-to-all-done.2.got_ref, bf16[8,2,2,256,256]{4,3,2,1,0:T(8,128)(2,1)S(1)} %copy-done, f32[8,9,8,128]{3,2,1,0:T(8,128)S(1)} %all_to_all.26.back_ref, ...), custom_call_target="tpu_custom_call" | custom-call | flops 268435456 | bytes 1048576 | tf_op jit(solution)/shard_map/pallas_call | solution.py:448
  51.8 14.4 %all_to_all.27 = f32[128,1,128]{2,1,0:T(1,128)S(1)} all-to-all(f32[128,1,128]{2,1,0:T(1,128)S(1)} %bitcast.8), channel_id=1, replica_groups=mesh['node_0'=4,'node_1'=4,'harm_0'=4,'harm_1'=2] {'node_0','node_1','ha..., dimensions={0} | all-to-all | bytes 131072 | tf_op jit(solution)/shard_map/all_to_all | solution.py:364
  66.2 1.0 %shard_map.120 = (f32[2,8,2048]{2,1,0:T(8,128)}, f32[2,8]{1,0:T(2,128)}, f32[1,1]{1,0:T(1,128)}) custom-call(f32[128,128]{1,0:T(8,128)S(1)} %bitcast.7, f32[2,8,2048]{2,1,0:T(8,128)S(1)} %get-tuple-element.27.refs_1_, f32[8,2,8,2048]{3,2,1,0:T(8,128)S(1)} %copy-done.1), custom_call_target="tpu_custom_call" | custom-call | flops 16777216 | bytes 1048576 | tf_op jit(solution)/shard_map/pallas_call | solution.py:458
Async XLA Ops:
  2.3 11.5 %copy-start.3 = (s32[2,8]{1,0:T(2,128)}, s32[2,8]{1,0:T(2,128)S(1)}, u32[]{:S(2)}) copy-start(s32[2,8]{1,0:T(2,128)S(1)} %get-tuple-element.17.names_ref) | copy-start | bytes 196
  2.3 13.2 %all-to-all-start = ((f32[8,6,8,128]{3,2,1,0:T(8,128)}), f32[8,6,8,128]{3,2,1,0:T(8,128)S(1)}, u32[]{:S(2)}, u32[]{:S(2)}) async-start(f32[8,6,8,128]{3,2,1,0:T(8,128)} %get-tuple-element.19), calls=%async_computation | async-start | bytes 393216 | tf_op jit(solution)/shard_map/all_to_all | solution.py:364
  9.1 8.1 %collective-permute-start = (s32[2,8]{1,0:T(2,128)S(1)}, s32[2,8]{1,0:T(2,128)S(1)}, u32[]{:S(2)}, u32[]{:S(2)}) collective-permute-start(s32[2,8]{1,0:T(2,128)S(1)} %get-tuple-element.17.names_ref), channel_id=1, source_target_pairs={{0,8},{8,16},{16,24},{24,32},{32,40},{40,48},{48,56},{56,64},{64,7... | collective-permute-start | bytes 200 | tf_op jit(solution)/shard_map/ppermute | solution.py:397
  29.3 8.7 %copy-start.1 = (f32[8,2,8,2048]{3,2,1,0:T(8,128)S(1)}, f32[8,2,8,2048]{3,2,1,0:T(8,128)}, u32[]{:S(2)}) copy-start(f32[8,2,8,2048]{3,2,1,0:T(8,128)} %refs_2_.1) | copy-start | bytes 3145732
  30.3 18.3 %all-to-all-start.2 = ((f32[16,2,4,8,128]{4,3,2,1,0:T(8,128)}), f32[16,2,4,8,128]{4,3,2,1,0:T(8,128)S(1)}, u32[]{:S(2)}, u32[]{:S(2)}) async-start(f32[16,2,4,8,128]{4,3,2,1,0:T(8,128)} %shard_map.116), calls=%async_computation.2 | async-start | bytes 1048576 | tf_op jit(solution)/shard_map/all_to_all | solution.py:364
  39.3 9.3 %copy-start.2 = (f32[1,128]{1,0:T(1,128)S(1)}, f32[1,128]{1,0:T(1,128)}, u32[]{:S(2)}) copy-start(f32[1,128]{1,0:T(1,128)} %shard_map.118.gram_ref) | copy-start | bytes 1540
  39.3 9.3 %copy-start.4 = (s32[2,8]{1,0:T(2,128)S(1)}, s32[2,8]{1,0:T(2,128)}, u32[]{:S(2)}) copy-start(s32[2,8]{1,0:T(2,128)} %get-tuple-element.18.where_ref) | copy-start | bytes 196
  48.6 2.2 %copy-start = (bf16[8,2,2,256,256]{4,3,2,1,0:T(8,128)(2,1)S(1)}, bf16[8,2,2,256,256]{4,3,2,1,0:T(8,128)(2,1)}, u32[]{:S(2)}) copy-start(bf16[8,2,2,256,256]{4,3,2,1,0:T(8,128)(2,1)} %shard_map.117.halves_ref) | copy-start | bytes 12582916

commit v5 on v4

--- a/solution.py
+++ b/solution.py
@@ -16,6 +16,8 @@
 HARM = ("harm_0", "harm_1")
 NODE = ("node_0", "node_1")
 NODE_HARM = ("node_0", "node_1", "harm_0", "harm_1")
+HARM_NODE = ("harm_0", "harm_1", "node_0", "node_1")
+ACROSS = ("node_1", "node_0")
 F32 = jnp.float32
 BF16 = jnp.bfloat16
 LANES = 128
@@ -53,6 +55,11 @@
     high, low = split(x)
     both = product(jnp.concatenate([high, low], axis=0), w_high)
     return both[:rows] + both[rows:] + product(high, w_low)
+
+
+def in_turn(group):
+    row = lax.div(group, lax.axis_size("node_1"))
+    return (group - row * lax.axis_size("node_1")) * lax.axis_size("node_0") + row
 
 
 def sublane_sum(x):
@@ -123,7 +130,7 @@
             name = names[j, b]
             group = lax.div(jnp.maximum(name, 0), blk)
             slot = jnp.where(name - group * blk == least[group], 0, 1)
-            where_ref[j, b] = jnp.where(name >= 0, 2 * group + slot, -1)
+            where_ref[j, b] = jnp.where(name >= 0, 2 * in_turn(group) + slot, -1)
     copies[0].wait()
     t_ref[...] = jnp.transpose(held[...])
     for copy in copies[2:]:
@@ -232,7 +239,7 @@
             code = back_ref[at, 8, 0:1, 0:1][0, 0].astype(jnp.int32)
             least = lax.div(code, CODE)
             for slot, b in enumerate((least, code - least * CODE)):
-                send_ref[group, slot] = back_ref[b, 4:8]
+                send_ref[in_turn(group), slot] = back_ref[b, 4:8]
 
 
 def halve_kernel(c_ref, out_ref, held, halves, in_sems, out_sems):
@@ -443,7 +450,7 @@
     send_named = call(
         select_kernel, struct(groups, 2, 4, h_dev, LANES), [VMEM], 1 << 34, limit=32 << 20
     )(back)
-    named = exchange(near(send_named), NODE)
+    named = exchange(near(send_named), ACROSS)
     gram = call(gram_kernel, far(1, LANES), [VMEM], 1 << 24, lanes)(krylov)
     image, send_sums = call(
         image_kernel,
@@ -453,7 +460,7 @@
         lanes,
         limit=32 << 20,
     )(near(where), near(named), near(halves), back, krylov, near(gram))
-    sums = near(exchange(send_sums, NODE_HARM))
+    sums = near(exchange(send_sums, HARM_NODE))
     count = world * h_dev * nodes_dev
     vector, proj, norm = call(
         lambda *refs: rest_kernel(count, *refs),

time: 67.7 us -> 68.2 us (level)
  no operation moved by 1% of the time
where the time goes in v5:
time: 68.2 us; the launch traced here: 67.7 us
  blocking collectives  26 us (38%)
  starting transfers between devices  19.2 us (28%)
  Pallas kernels  14 us (21%)
  waiting for transfers between devices  5.5 us (8%)
  local copies, waits for them, and re-layouts  2.21 us (3%)
  between operations  0.73 us (1%)
    all_to_all x2, blocking collectives, exchange(): return lax.all_to_all(x, axes, split_axis=0, concat_axis=0, tiled=True)  26 us
    all_to_all x2, starting transfers between devices, exchange(): return lax.all_to_all(x, axes, split_axis=0, concat_axis=0, tiled=True)  14.6 us
    all_to_all x2, waiting for transfers between devices, exchange(): return lax.all_to_all(x, axes, split_axis=0, concat_axis=0, tiled=True)  5.5 us
    ppermute x1, starting transfers between devices, per_device(): named_by = lax.ppermute(near(names), NODE_HARM, pairs)  4.64 us
    pallas_call x1, Pallas kernels, per_device(): call(halve_kernel, far(blk, NEIGH, 2, BS, BS, dtype=BF16), [ANY], 1 << 24...  3.66 us
    unnamed x10, local copies, waits for them, and re-layouts  2.21 us
    pallas_call x1, Pallas kernels, per_device(): call(turn_kernel, (struct(BS, BS), far(NEIGH, blk, dtype=jnp.int32), stru...  1.79 us
    pallas_call x1, Pallas kernels, per_device(): call(pack_kernel, (far(blk, 6, h_dev, LANES), struct(NEIGH, blk, dtype=jn...  1.65 us
  transfers between devices with their start and end apart: 3, of which 1 were waited for; matrix products, arithmetic and copies ran while one was open for 0% of the time, Pallas kernels for 12%

profile of v5, /device:TPU:1, one launch (start us, length us, event | category | flops | bytes accessed | tf_op | source)
XLA Modules:
  0.0 67.7 jit_solution(2347791995890571589)
XLA Ops:
  0.6 1.6 %shard_map.112 = (f32[8,6,8,128]{3,2,1,0:T(8,128)}, s32[2,8]{1,0:T(2,128)S(1)}) custom-call(f32[8,2,8,2048]{3,2,1,0:T(8,128)} %refs_2_.1, f32[8,2048]{1,0:T(8,128)} %cond_ref.1, s32[2,8]{1,0:T(2,128)} %bitcast.9, s32[2,8]{1,0:T(2,128)} %bitcast.10), custom_call_target="tpu_custom_call" | custom-call | flops 1048576 | bytes 1048576 | tf_op jit(solution)/shard_map/pallas_call | solution.py:384
  2.3 0.0 copy-start.3
  2.3 6.8 %all-to-all-start = ((f32[8,6,8,128]{3,2,1,0:T(8,128)}), f32[8,6,8,128]{3,2,1,0:T(8,128)S(1)}, u32[]{:S(2)}, u32[]{:S(2)}) async-start(f32[8,6,8,128]{3,2,1,0:T(8,128)} %get-tuple-element.19), calls=%async_computation | async-start | bytes 393216 | tf_op jit(solution)/shard_map/all_to_all | solution.py:371
  9.1 4.6 %collective-permute-start = (s32[2,8]{1,0:T(2,128)S(1)}, s32[2,8]{1,0:T(2,128)S(1)}, u32[]{:S(2)}, u32[]{:S(2)}) collective-permute-start(s32[2,8]{1,0:T(2,128)S(1)} %get-tuple-element.17.names_ref), channel_id=1, source_target_pairs={{0,8},{8,16},{16,24},{24,32},{32,40},{40,48},{48,56},{56,64},{64,7... | collective-permute-start | bytes 200 | tf_op jit(solution)/shard_map/ppermute | solution.py:404
  13.8 0.0 copy-done.3
  13.8 1.8 %shard_map.113 = (f32[256,256]{1,0:T(8,128)S(1)}, s32[2,8]{1,0:T(2,128)}, f32[2048]{0:T(1024)S(1)}, bf16[2,128,128]{2,1,0:T(8,128)(2,1)S(1)}, bf16[2,128,128]{2,1,0:T(8,128)(2,1)S(1)}) custom-call(s32[2,8]{1,0:T(2,128)} %copy-done.3, f32[8,256,256]{2,1,0:T(8,128)} %diag_ref.1, f32[2048]{0:T(1024)} %cap_ref.1, bf16[2,128,128]{2,1,0:T(8,128)(2,1)} %constant.4.clone.high_ref, ...), custom_call_target="tpu_custom_call" | custom-call | flops 16777216 | bytes 1048576 | tf_op jit(solution)/shard_map/pallas_call | solution.py:406
  15.6 0.0 all-to-all-done.got_ref
  15.6 1.6 %shard_map.114 = (f32[128,256]{1,0:T(8,128)S(1)}, f32[128,256]{1,0:T(8,128)S(1)}) custom-call(f32[8,6,8,128]{3,2,1,0:T(8,128)S(1)} %all-to-all-done.got_ref, f32[256,256]{1,0:T(8,128)S(1)} %get-tuple-element.20.t_ref), custom_call_target="tpu_custom_call" | custom-call | flops 536870912 | bytes 1048576 | tf_op jit(solution)/shard_map/pallas_call | solution.py:426
  17.2 0.0 collective-permute-done.names_ref
  17.2 1.2 %shard_map.115 = f32[8,9,8,128]{3,2,1,0:T(8,128)} custom-call(f32[8,6,8,128]{3,2,1,0:T(8,128)S(1)} %all-to-all-done.got_ref, f32[128,256]{1,0:T(8,128)S(1)} %get-tuple-element.21.u_ref, f32[128,256]{1,0:T(8,128)S(1)} %get-tuple-element.22.direct_ref, f32[2048]{0:T(1024)S(1)} %get-tuple-element.23.cap_ref, ...), custom_call_target="tpu_custom_call" | custom-call | flops 134217728 | bytes 1048576 | tf_op jit(solution)/shard_map/pallas_call | solution.py:433
  18.4 11.0 %all_to_all.26.back_ref = f32[8,9,8,128]{3,2,1,0:T(8,128)S(1)} all-to-all(f32[8,9,8,128]{3,2,1,0:T(8,128)} %shard_map.115), channel_id=1, replica_groups=mesh['node_0'=4,'node_1'=4,'harm_0'=4,'harm_1'=2] {'harm_0','harm_1'}, dimensions={0} | all-to-all | bytes 589824 | tf_op jit(solution)/shard_map/all_to_all | solution.py:371
  29.3 0.0 copy-start.1
  29.3 0.9 %shard_map.116 = f32[16,2,4,8,128]{4,3,2,1,0:T(8,128)} custom-call(f32[8,9,8,128]{3,2,1,0:T(8,128)S(1)} %all_to_all.26.back_ref), custom_call_target="tpu_custom_call" | custom-call | flops 17179869184 | bytes 1048576 | tf_op jit(solution)/shard_map/pallas_call | solution.py:450
  30.3 7.8 %all-to-all-start.2 = ((f32[16,2,4,8,128]{4,3,2,1,0:T(8,128)}), f32[16,2,4,8,128]{4,3,2,1,0:T(8,128)S(1)}, u32[]{:S(2)}, u32[]{:S(2)}) async-start(f32[16,2,4,8,128]{4,3,2,1,0:T(8,128)} %shard_map.116), calls=%async_computation.2 | async-start | bytes 1048576 | tf_op jit(solution)/shard_map/all_to_all | solution.py:371
  38.1 0.0 copy-done.1
  38.1 1.2 %shard_map.118.gram_ref = f32[1,128]{1,0:T(1,128)} custom-call(f32[8,2,8,2048]{3,2,1,0:T(8,128)S(1)} %copy-done.1), custom_call_target="tpu_custom_call" | custom-call | flops 16777216 | bytes 1048576 | tf_op jit(solution)/shard_map/pallas_call | solution.py:454
  39.3 0.0 copy-start.2
  39.3 0.0 copy-start.4
  39.3 3.7 %shard_map.117.halves_ref = bf16[8,2,2,256,256]{4,3,2,1,0:T(8,128)(2,1)} custom-call(f32[8,2,256,256]{3,2,1,0:T(8,128)} %c_ref.1), custom_call_target="tpu_custom_call" | custom-call | flops 16777216 | bytes 1048576 | tf_op jit(solution)/shard_map/pallas_call | solution.py:437
  42.9 5.5 %all-to-all-done.2.got_ref = f32[16,2,4,8,128]{4,3,2,1,0:T(8,128)S(1)} async-done(((f32[16,2,4,8,128]{4,3,2,1,0:T(8,128)}), f32[16,2,4,8,128]{4,3,2,1,0:T(8,128)S(1)}, u32[]{:S(2)}, u32[]{:S(2)}) %all-to-all-start.2) | async-done | bytes 524320 | tf_op jit(solution)/shard_map/all_to_all | solution.py:371
  48.4 0.0 copy-done.2
  48.4 0.0 copy-done.4
  48.4 0.0 copy-start
  48.4 2.2 %copy-done = bf16[8,2,2,256,256]{4,3,2,1,0:T(8,128)(2,1)S(1)} copy-done((bf16[8,2,2,256,256]{4,3,2,1,0:T(8,128)(2,1)S(1)}, bf16[8,2,2,256,256]{4,3,2,1,0:T(8,128)(2,1)}, u32[]{:S(2)}) %copy-start) | copy-done | bytes 4194328
  50.6 1.0 %shard_map.119 = (f32[2,8,2048]{2,1,0:T(8,128)S(1)}, f32[128,128]{1,0:T(8,128)S(1)}) custom-call(s32[2,8]{1,0:T(2,128)S(1)} %copy-done.4, f32[16,2,4,8,128]{4,3,2,1,0:T(8,128)S(1)} %all-to-all-done.2.got_ref, bf16[8,2,2,256,256]{4,3,2,1,0:T(8,128)(2,1)S(1)} %copy-done, f32[8,9,8,128]{3,2,1,0:T(8,128)S(1)} %all_to_all.26.back_ref, ...), custom_call_target="tpu_custom_call" | custom-call | flops 268435456 | bytes 1048576 | tf_op jit(solution)/shard_map/pallas_call | solution.py:455
  51.6 15.1 %all_to_all.27 = f32[128,1,128]{2,1,0:T(1,128)S(1)} all-to-all(f32[128,1,128]{2,1,0:T(1,128)S(1)} %bitcast.8), channel_id=1, replica_groups=mesh['node_0'=4,'node_1'=4,'harm_0'=4,'harm_1'=2] {'harm_0','harm_1','no..., dimensions={0} | all-to-all | bytes 131072 | tf_op jit(solution)/shard_map/all_to_all | solution.py:371
  66.7 1.0 %shard_map.120 = (f32[2,8,2048]{2,1,0:T(8,128)}, f32[2,8]{1,0:T(2,128)}, f32[1,1]{1,0:T(1,128)}) custom-call(f32[128,128]{1,0:T(8,128)S(1)} %bitcast.7, f32[2,8,2048]{2,1,0:T(8,128)S(1)} %get-tuple-element.27.refs_1_, f32[8,2,8,2048]{3,2,1,0:T(8,128)S(1)} %copy-done.1), custom_call_target="tpu_custom_call" | custom-call | flops 16777216 | bytes 1048576 | tf_op jit(solution)/shard_map/pallas_call | solution.py:465
Async XLA Ops:
  2.3 11.5 %copy-start.3 = (s32[2,8]{1,0:T(2,128)}, s32[2,8]{1,0:T(2,128)S(1)}, u32[]{:S(2)}) copy-start(s32[2,8]{1,0:T(2,128)S(1)} %get-tuple-element.17.names_ref) | copy-start | bytes 196
  2.3 13.3 %all-to-all-start = ((f32[8,6,8,128]{3,2,1,0:T(8,128)}), f32[8,6,8,128]{3,2,1,0:T(8,128)S(1)}, u32[]{:S(2)}, u32[]{:S(2)}) async-start(f32[8,6,8,128]{3,2,1,0:T(8,128)} %get-tuple-element.19), calls=%async_computation | async-start | bytes 393216 | tf_op jit(solution)/shard_map/all_to_all | solution.py:371
  9.1 8.1 %collective-permute-start = (s32[2,8]{1,0:T(2,128)S(1)}, s32[2,8]{1,0:T(2,128)S(1)}, u32[]{:S(2)}, u32[]{:S(2)}) collective-permute-start(s32[2,8]{1,0:T(2,128)S(1)} %get-tuple-element.17.names_ref), channel_id=1, source_target_pairs={{0,8},{8,16},{16,24},{24,32},{32,40},{40,48},{48,56},{56,64},{64,7... | collective-permute-start | bytes 200 | tf_op jit(solution)/shard_map/ppermute | solution.py:404
  29.3 8.7 %copy-start.1 = (f32[8,2,8,2048]{3,2,1,0:T(8,128)S(1)}, f32[8,2,8,2048]{3,2,1,0:T(8,128)}, u32[]{:S(2)}) copy-start(f32[8,2,8,2048]{3,2,1,0:T(8,128)} %refs_2_.1) | copy-start | bytes 3145732
  30.3 18.2 %all-to-all-start.2 = ((f32[16,2,4,8,128]{4,3,2,1,0:T(8,128)}), f32[16,2,4,8,128]{4,3,2,1,0:T(8,128)S(1)}, u32[]{:S(2)}, u32[]{:S(2)}) async-start(f32[16,2,4,8,128]{4,3,2,1,0:T(8,128)} %shard_map.116), calls=%async_computation.2 | async-start | bytes 1048576 | tf_op jit(solution)/shard_map/all_to_all | solution.py:371
  39.3 9.2 %copy-start.2 = (f32[1,128]{1,0:T(1,128)S(1)}, f32[1,128]{1,0:T(1,128)}, u32[]{:S(2)}) copy-start(f32[1,128]{1,0:T(1,128)} %shard_map.118.gram_ref) | copy-start | bytes 1540
  39.3 9.2 %copy-start.4 = (s32[2,8]{1,0:T(2,128)S(1)}, s32[2,8]{1,0:T(2,128)}, u32[]{:S(2)}) copy-start(s32[2,8]{1,0:T(2,128)} %get-tuple-element.18.where_ref) | copy-start | bytes 196
  48.4 2.2 %copy-start = (bf16[8,2,2,256,256]{4,3,2,1,0:T(8,128)(2,1)S(1)}, bf16[8,2,2,256,256]{4,3,2,1,0:T(8,128)(2,1)}, u32[]{:S(2)}) copy-start(bf16[8,2,2,256,256]{4,3,2,1,0:T(8,128)(2,1)} %shard_map.117.halves_ref) | copy-start | bytes 12582916
